TPU v7x, 128 devices: a whole 4x4x4 slice. The times are simulated.
128 devices in a mesh: section: 16 (over z, x_hi, core), tm: 8 (over y, x_lo).
Axes of the slice: x: 4 (x_hi: 2, x_lo: 2; x = x_hi * 2 + x_lo), y: 4, z: 4, core: 2. Of those that a mesh axis runs over, the one named last changes fastest.
Arguments:
- frames: bfloat16 [4, 512, 1024], P(None, 'tm'), may hold values from -6 to 6, as said below
- lengths: int32 [4], replicated, may hold values from 128 to 512
- ffn_gain: float32 [16, 1024], P('section'), may hold values from 0.1 to 1.9
- ffn_up: bfloat16 [16, 1024, 2048], P('section'), may hold values from -0.1875 to 0.1875
- ffn_down: bfloat16 [16, 2048, 1024], P('section'), may hold values from -0.125 to 0.125
- attn_gain: float32 [16, 1024], P('section'), may hold values from 0.1 to 1.9
- query_weight: bfloat16 [16, 1024, 1024], P('section'), may hold values from -8 to 8
- key_weight: bfloat16 [16, 1024, 1024], P('section'), may hold values from -0.1875 to 0.1875
- value_weight: bfloat16 [16, 1024, 1024], P('section'), may hold values from -0.1875 to 0.1875
- out_weight: bfloat16 [16, 1024, 1024], P('section'), may hold values from -0.1875 to 0.1875
- conv_gain: float32 [16, 1024], P('section'), may hold values from 0.1 to 1.9
- expand_weight: bfloat16 [16, 1024, 2048], P('section'), may hold values from -0.1875 to 0.1875
- depth_weight: float32 [16, 31, 1024], P('section'), may hold values from -1 to 1
- depth_gain: float32 [16, 1024], P('section'), may hold values from 0.1 to 1.9
- norm_shift: float32 [16, 1024], P('section'), may hold values from -0.5 to 0.5
- shrink_weight: bfloat16 [16, 1024, 1024], P('section'), may hold values from -0.1875 to 0.1875
- final_gain: float32 [16, 1024], P('section'), may hold values from 0.1 to 1.9
Outputs:
- hidden_states: bfloat16 [16, 4, 512, 1024], P('section', None, 'tm')
Inputs may be any that keep to these rules, and one draw needn't show every extreme that they name: `frames`: input features of order one.
All inputs are finite; a program needn't handle non-finite values.
Results may differ from a plain program's by a relative error of at most 0.02.
Values may be sent and summed in bfloat16 or wider, within the bound.
A program may use at most 128 MiB of HBM per device.

v0:
```python
import math

import jax
import jax.numpy as jnp
from jax import lax
from jax.sharding import PartitionSpec as P

HEADS = 16


EPS = 1e-05


def extended(shard, sides, width):
    for axis, dim in sides:
        peers, length = (lax.axis_size(axis), shard.shape[dim])
        up = [(i, (i + 1) % peers) for i in range(peers - 1)]
        down = [(j, i) for i, j in up]
        last = lax.slice_in_dim(shard, length - width, length, axis=dim)
        initial = lax.slice_in_dim(shard, 0, width, axis=dim)
        before = lax.ppermute(last, axis, up)
        after = lax.ppermute(initial, axis, down)
        shard = jnp.concatenate([before, shard, after], axis=dim)
    return shard


def passed_along(shard, axis, by):
    peers = lax.axis_size(axis)
    pairs = [(i, i + by) for i in range(peers) if 0 <= i + by < peers]
    return lax.ppermute(shard, axis, pairs)


def normalize(value, gain):
    mean = jnp.mean(value, axis=-1, keepdims=True)
    centred = value - mean
    spread = jnp.mean(centred * centred, axis=-1, keepdims=True)
    return centred * lax.rsqrt(spread + EPS) * gain


def body(
    frames,
    lengths,
    ffn_gain,
    ffn_up,
    ffn_down,
    attn_gain,
    query_weight,
    key_weight,
    value_weight,
    out_weight,
    conv_gain,
    expand_weight,
    depth_weight,
    depth_gain,
    norm_shift,
    shrink_weight,
    final_gain,
):
    sections = lax.axis_size("section")
    groups = lax.axis_size("tm")
    section_index = lax.axis_index("section")
    group_index = lax.axis_index("tm")
    micro, rows, width = frames.shape
    whole = rows * groups
    heads = HEADS
    head = width // heads
    kernel = depth_weight.shape[1]
    rim = kernel // 2
    scale = 1.0 / math.sqrt(head)
    gain_ffn = ffn_gain[0]
    w_up = ffn_up[0]
    w_down = ffn_down[0]
    gain_a = attn_gain[0]
    w_query = query_weight[0]
    w_key = key_weight[0]
    w_value = value_weight[0]
    w_out = out_weight[0]
    gain_c = conv_gain[0]
    w_expand = expand_weight[0]
    w_depth = depth_weight[0]
    gain_depth = depth_gain[0]
    bias_depth = norm_shift[0]
    w_shrink = shrink_weight[0]
    gain_f = final_gain[0]
    local_pos = group_index * rows + jnp.arange(rows, dtype=jnp.int32)
    zero_rows = jnp.zeros((rows, width), jnp.bfloat16)
    zero_mid = jnp.zeros((rows, width), jnp.float32)

    def tick(step, carry):
        incoming, gathered = carry
        offset = step - section_index
        active = (offset >= 0) & (offset < micro)
        slot = jnp.clip(offset, 0, micro - 1)
        fresh = lax.dynamic_index_in_dim(frames, slot, 0, keepdims=False)
        inputs = jnp.where(section_index == 0, fresh, incoming)
        length = jnp.sum(jnp.where(jnp.arange(micro, dtype=jnp.int32) == slot, lengths, 0))

        def project():
            ffn_normed = normalize(inputs.astype(jnp.float32), gain_ffn).astype(jnp.bfloat16)
            inner = jax.nn.silu(
                jnp.dot(ffn_normed, w_up, preferred_element_type=jnp.float32)
            ).astype(jnp.bfloat16)
            start = inputs.astype(jnp.float32) + 0.5 * jnp.dot(
                inner, w_down, preferred_element_type=jnp.float32
            )
            normed = normalize(start, gain_a).astype(jnp.bfloat16)
            q_all, k_all, v_all = tuple(
                (
                    jnp.dot(normed, weight, preferred_element_type=jnp.float32).astype(jnp.bfloat16)
                    for weight in (w_query, w_key, w_value)
                )
            )
            return (start, q_all, k_all, v_all)

        start, queries, keys, values = lax.cond(
            active, project, lambda: (zero_mid, zero_rows, zero_rows, zero_rows)
        )
        g_query, g_key, g_value = (
            lax.all_to_all(queries, "tm", split_axis=1, concat_axis=0, tiled=True),
            lax.all_to_all(keys, "tm", split_axis=1, concat_axis=0, tiled=True),
            lax.all_to_all(values, "tm", split_axis=1, concat_axis=0, tiled=True),
        )
        local_heads = g_query.shape[1] // head
        span = 512

        def attend_groups():
            seen = jnp.arange(whole, dtype=jnp.int32) < length
            k_heads = g_key.reshape(whole, local_heads, head)
            v_heads = g_value.reshape(whole, local_heads, head)
            q_blocks = g_query.reshape(whole // span, span, local_heads, head)

            def one_block(q_block):
                scores = (
                    jnp.einsum("qgd,kgd->gqk", q_block, k_heads, preferred_element_type=jnp.float32)
                    * scale
                )
                scores = jnp.where(seen[None, None, :], scores, -1e30)
                peak = jnp.max(scores, axis=-1, keepdims=True)
                weights_h = jnp.exp(scores - peak)
                total = jnp.sum(weights_h, axis=-1, keepdims=True)
                mixed = jnp.einsum(
                    "gqk,kgd->qgd",
                    weights_h.astype(jnp.bfloat16),
                    v_heads,
                    preferred_element_type=jnp.float32,
                )
                mixed = mixed / jnp.transpose(total, (1, 0, 2))
                return mixed.astype(jnp.bfloat16).reshape(span, local_heads * head)

            return lax.map(one_block, q_blocks).reshape(whole, local_heads * head)

        grouped = lax.cond(
            active, attend_groups, lambda: jnp.zeros((whole, local_heads * head), jnp.bfloat16)
        )
        context = lax.all_to_all(grouped, "tm", split_axis=0, concat_axis=1, tiled=True)

        def conv_front():
            mid = start + jnp.dot(context, w_out, preferred_element_type=jnp.float32)
            conv_in = normalize(mid, gain_c).astype(jnp.bfloat16)
            expanded = jnp.dot(conv_in, w_expand, preferred_element_type=jnp.float32)
            keep = (local_pos < length).astype(jnp.float32)
            glu = expanded[:, :width] * jax.nn.sigmoid(expanded[:, width:]) * keep[:, None]
            return (mid, glu.astype(jnp.bfloat16))

        mid, glu = lax.cond(active, conv_front, lambda: (zero_mid, zero_rows))
        padded = extended(glu, (("tm", 0),), rim)

        def conv_back():
            widened = padded.astype(jnp.float32)
            depth = jnp.zeros((rows, width), jnp.float32)
            for offset_j in range(kernel):
                depth = depth + widened[offset_j : offset_j + rows] * w_depth[offset_j]
            shifted = normalize(depth, gain_depth) + bias_depth
            swished = (shifted * jax.nn.sigmoid(shifted)).astype(jnp.bfloat16)
            closing = mid + jnp.dot(swished, w_shrink, preferred_element_type=jnp.float32)
            return normalize(closing, gain_f).astype(jnp.bfloat16)

        result = lax.cond(active, conv_back, lambda: zero_rows)
        previous = lax.dynamic_index_in_dim(gathered, slot, 0, keepdims=False)
        gathered = lax.dynamic_update_index_in_dim(
            gathered, jnp.where(active, result, previous), slot, 0
        )
        incoming = passed_along(result, "section", 1)
        return (incoming, gathered)

    start_outs = jnp.zeros((micro, rows, width), jnp.bfloat16)
    final_in, hidden_states = lax.fori_loop(0, micro + sections - 1, tick, (zero_rows, start_outs))
    return hidden_states[None]


def solution(mesh):
    return jax.shard_map(
        body,
        mesh=mesh,
        in_specs=(
            P(None, "tm", None),
            P(),
            P("section", None),
            P("section", None, None),
            P("section", None, None),
            P("section", None),
            P("section", None, None),
            P("section", None, None),
            P("section", None, None),
            P("section", None, None),
            P("section", None),
            P("section", None, None),
            P("section", None, None),
            P("section", None),
            P("section", None),
            P("section", None, None),
            P("section", None),
        ),
        out_specs=P("section", None, "tm", None),
        check_vma=False,
    )
```

profile of v0, /device:TPU:111, one launch (start us, length us, event | category | flops | bytes accessed | tf_op | source)
XLA Modules:
  0.0 1491.1 jit_solution(9825759738350076696)
XLA Ops:
  2.5 1488.7 %while.21 = (s32[]{:T(128)}, bf16[64,1024]{1,0:T(8,128)(2,1)S(1)}, bf16[4,64,1024]{2,1,0:T(8,128)(2,1)}, s32[]{:T(128)}, s32[4]{0:T(128)}, /*index=5*/pred[]{:T(...) while((s32[]{:T(128)}, bf16[64,1024]{1,0:T(8,128)(2,1)S(1)}, ...), condition=%wide.region_22.23_spmd.clone, body=%wide.region_0.22_spmd.clone.sunk | while | flops 1626031104 | bytes 78909456 | solution.py:187
  105.8 11.8 collective-permute-done.2
  165.7 11.8 collective-permute-done.2
  225.6 11.8 collective-permute-done.2
  285.5 11.8 collective-permute-done.2
  345.3 11.8 collective-permute-done.2
  405.2 11.8 collective-permute-done.2
  465.1 11.8 collective-permute-done.2
  525.0 11.8 collective-permute-done.2
  584.8 11.8 collective-permute-done.2
  644.7 12.1 collective-permute-done.2
  705.1 12.1 collective-permute-done.2
  765.4 12.0 collective-permute-done.2
  825.5 11.8 collective-permute-done.2
  885.1 278.9 %collective-permute-done.2 = bf16[64,1024]{1,0:T(8,128)(2,1)S(1)} collective-permute-done((bf16[64,1024]{1,0:T(8,128)(2,1)S(1)}, bf16[64,1024]{1,0:T(8,128)(2,1)S(1)}, u32[]{:S(2)}, u32[]{:S(2)}) %collective-permute-start.2) | collective-permute-done | bytes 131104 | tf_op jit(solution)/shard_map/while/body/eval_jaxpr/ppermute | solution.py:30
  1163.9 10.7 conditional.12
  1214.7 8.2 conditional.14
  1235.7 13.2 collective-permute-done.2
  1248.9 10.7 conditional.12
  1320.6 13.2 collective-permute-done.2
  1333.8 10.7 conditional.12
  1384.5 8.2 conditional.14
  1405.5 12.7 collective-permute-done.2
  1418.2 10.7 conditional.12
  (1090 shorter events, 1066.6 us)
Async XLA Ops:
  12.2 9.2 all-to-all-start.1
  48.1 9.6 collective-permute-start.2
  58.5 9.1 all-to-all-start
  103.9 13.8 collective-permute-start.2
  163.7 13.8 collective-permute-start.2
  223.6 13.8 collective-permute-start.2
  283.5 13.8 collective-permute-start.2
  343.3 13.8 collective-permute-start.2
  403.2 13.8 collective-permute-start.2
  463.1 13.8 collective-permute-start.2
  523.0 13.8 collective-permute-start.2
  582.8 13.8 collective-permute-start.2
  642.7 14.1 collective-permute-start.2
  657.6 9.3 all-to-all-start
  703.1 14.1 collective-permute-start.2
  717.9 9.3 all-to-all-start
  763.4 14.0 collective-permute-start.2
  778.1 9.2 all-to-all-start
  823.5 13.8 collective-permute-start.2
  883.1 280.9 %collective-permute-start.2 = (bf16[64,1024]{1,0:T(8,128)(2,1)S(1)}, bf16[64,1024]{1,0:T(8,128)(2,1)S(1)}, u32[]{:S(2)}, u32[]{:S(2)}) collective-permute-start(bf16[64,1024]{1,0:T(8,128)(2,1)S(1)} %get-tuple-element.1026), channel_id=1, source_target_pairs={{0,8},{8,16},{16,24},{24,32},{32,40},{40,48},{48,56},{56,64},{64,7... | collective-permute-start | bytes 393224 | tf_op jit(solution)/shard_map/while/body/eval_jaxpr/ppermute | solution.py:30
  1233.7 15.2 %collective-permute-start.2 = (bf16[64,1024]{1,0:T(8,128)(2,1)S(1)}, bf16[64,1024]{1,0:T(8,128)(2,1)S(1)}, u32[]{:S(2)}, u32[]{:S(2)}) collective-permute-start(bf16[64,1024]{1,0:T(8,128)(2,1)S(1)} %get-tuple-element.1026), channel_id=1, source_target_pairs={{0,8},{8,16},{16,24},{24,32},{32,40},{40,48},{48,56},{56,64},{64,7... | collective-permute-start | bytes 393224 | tf_op jit(solution)/shard_map/while/body/eval_jaxpr/ppermute | solution.py:30
  1318.6 15.2 %collective-permute-start.2 = (bf16[64,1024]{1,0:T(8,128)(2,1)S(1)}, bf16[64,1024]{1,0:T(8,128)(2,1)S(1)}, u32[]{:S(2)}, u32[]{:S(2)}) collective-permute-start(bf16[64,1024]{1,0:T(8,128)(2,1)S(1)} %get-tuple-element.1026), channel_id=1, source_target_pairs={{0,8},{8,16},{16,24},{24,32},{32,40},{40,48},{48,56},{56,64},{64,7... | collective-permute-start | bytes 393224 | tf_op jit(solution)/shard_map/while/body/eval_jaxpr/ppermute | solution.py:30
  1403.5 14.7 collective-permute-start.2
  1429.6 9.1 all-to-all-start
  (262 other events, 2580.4 us)
where the time goes:
time: 1500 us; the launch traced here: 1490 us
  waiting for transfers between devices  732 us (49%)
  starting transfers between devices  543 us (36%)
  local copies, waits for them, and re-layouts  89.2 us (6%)
  matrix products  70 us (5%)
  other arithmetic  52.2 us (3%)
    ppermute x19, waiting for transfers between devices, passed_along(): return lax.ppermute(shard, axis, pairs)  482 us
    all_to_all x19, starting transfers between devices, tick(): lax.all_to_all(queries, 'tm', split_axis=1, concat_axis=0, tiled=True)  104 us
    all_to_all x19, starting transfers between devices, tick(): lax.all_to_all(keys, 'tm', split_axis=1, concat_axis=0, tiled=True)  98.6 us
    all_to_all x19, starting transfers between devices, tick(): lax.all_to_all(grouped, 'tm', split_axis=0, concat_axis=1, tiled=True)  98.5 us
    all_to_all x19, starting transfers between devices, tick(): lax.all_to_all(values, 'tm', split_axis=1, concat_axis=0, tiled=True)  98.2 us
    all_to_all x19, waiting for transfers between devices, tick(): lax.all_to_all(grouped, 'tm', split_axis=0, concat_axis=1, tiled=True)  69.7 us
    ppermute x19, starting transfers between devices, extended(): before = lax.ppermute(last, axis, up)  65.3 us
    all_to_all x19, waiting for transfers between devices, tick(): lax.all_to_all(keys, 'tm', split_axis=1, concat_axis=0, tiled=True)  57.3 us
  transfers between devices with their start and end apart: 133, of which 114 were waited for; matrix products, arithmetic and copies ran while one was open for 5% of the time, Pallas kernels for 0%

commit v1 on v0

v1 whole, which is shorter than its diff:
```python
import functools

import jax
import jax.numpy as jnp
from jax import lax
from jax.experimental import pallas as pl
from jax.experimental.pallas import tpu as pltpu
from jax.sharding import PartitionSpec as P

MESH = pl.DeviceIdType.MESH
F32 = jnp.float32
BF16 = jnp.bfloat16
EPS = 1e-05
D = 1024
FF = 2048
HEADS = 16
ROWS = 256
LEN = 512
TAPS = 31
UTTS = 4
STAGES = 8
PIECE = 64
PIECES = ROWS // PIECE
SHAPES = ((D, FF), (FF, D), (D, D), (D, D), (D, D), (D, D), (D, 2 * D), (D, D))


def sigmoid(v):
    return 0.5 * jnp.tanh(0.5 * v) + 0.5


def normed(v, gain):
    mean = jnp.mean(v, axis=-1, keepdims=True)
    centred = v - mean
    spread = jnp.mean(centred * centred, axis=-1, keepdims=True)
    return centred * lax.rsqrt(spread + EPS) * gain


def dot(a, b):
    return jnp.dot(a, b, preferred_element_type=F32)


def block_kernel(
    lengths,
    frames,
    ffn_gain,
    attn_gain,
    conv_gain,
    depth_gain,
    norm_shift,
    final_gain,
    depth_weight,
    h_up,
    h_down,
    h_key,
    h_value,
    h_query,
    h_out,
    h_expand,
    h_shrink,
    out,
    w_up,
    w_down,
    w_key,
    w_value,
    w_query,
    w_out,
    w_expand,
    w_shrink,
    vec,
    taps,
    xs,
    act,
    wide,
    res,
    kv,
    rim_out,
    rim_in,
    padded,
    depth,
    local_sem,
    push_sem,
    pull_sem,
    x_send,
    x_recv,
    out_send,
    out_recv,
    kv_send,
    kv_recv,
    rim_send,
    rim_recv,
    frame_send,
):
    s = lax.axis_index("section")
    t = lax.axis_index("tm")
    k = s // 2
    c = lax.rem(s, 2)
    u = t // 2
    side = 1 - lax.rem(k, 2)
    active = lax.rem(t, 2) == side
    partner = {"section": 2 * k + 1 - c, "tm": t}
    here = {"section": s, "tm": t}
    del here

    hbm = (h_up, h_down, h_key, h_value, h_query, h_out, h_expand, h_shrink)
    vmem = (w_up, w_down, w_key, w_value, w_query, w_out, w_expand, w_shrink)
    small = (ffn_gain, attn_gain, conv_gain, depth_gain, norm_shift, final_gain)

    def sources():
        pairs = [(small[i], vec.at[c, i]) for i in range(6)]
        pairs += [(depth_weight.at[0], taps.at[c])]
        pairs += [(hbm[i].at[0], vmem[i].at[c]) for i in range(8)]
        return pairs

    def arrivals(slot):
        refs = [vec.at[slot, i] for i in range(6)] + [taps.at[slot]]
        return refs + [vmem[i].at[slot] for i in range(8)]

    def local(i):
        src, dst = sources()[i]
        return pltpu.make_async_copy(src, dst, local_sem.at[i])

    def push(i):
        src, dst = sources()[i]
        return pltpu.make_async_remote_copy(
            src, dst, push_sem.at[i], pull_sem.at[i], device_id=partner, device_id_type=MESH
        )

    def pull(i, slot):
        ref = arrivals(slot)[i]
        return pltpu.make_async_remote_copy(
            ref, ref, push_sem.at[i], pull_sem.at[i], device_id=partner, device_id_type=MESH
        )

    ORDER = (0, 7, 8, 1, 9, 10, 11, 12, 2, 13, 3, 4, 6, 14, 5)

    @pl.when(active)
    def _():
        for i in ORDER:
            local(i).start()
        for i in ORDER:
            push(i).start()

    def frame_copy(v):
        return pltpu.make_async_remote_copy(
            frames.at[v],
            xs.at[0, pl.ds(pl.multiple_of(lax.rem(t, 4) * PIECE, PIECE), PIECE)],
            frame_send.at[v],
            x_recv.at[lax.rem(t, 4)],
            device_id={"section": s, "tm": 2 * v + 1},
            device_id_type=MESH,
        )

    def frame_local(v):
        return pltpu.make_async_copy(
            frames.at[v],
            xs.at[0, pl.ds(pl.multiple_of(lax.rem(t, 4) * PIECE, PIECE), PIECE)],
            x_recv.at[lax.rem(t, 4)],
        )

    sends_frames = (k == 0) & (t // 4 == c)
    for v in range(UTTS):

        @pl.when(sends_frames & (t != 2 * v + 1))
        def _(v=v):
            frame_copy(v).start()

        @pl.when(sends_frames & (t == 2 * v + 1))
        def _(v=v):
            frame_local(v).start()

    def piece_rows(j):
        return pl.ds(j * PIECE, PIECE)

    def forward(j):
        return pltpu.make_async_remote_copy(
            xs.at[2, piece_rows(j)],
            xs.at[0, piece_rows(j)],
            x_send.at[j],
            x_recv.at[j],
            device_id={"section": lax.rem(s + 2, 16), "tm": 2 * u + 1 - side},
            device_id_type=MESH,
        )

    def scatter(slot, j):
        return pltpu.make_async_remote_copy(
            xs.at[slot + 1, piece_rows(j)],
            out.at[0, u],
            out_send.at[slot, j],
            out_recv.at[u],
            device_id={"section": 2 * k + slot, "tm": 4 * c + j},
            device_id_type=MESH,
        )

    def scatter_local(slot, j):
        return pltpu.make_async_copy(xs.at[slot + 1, piece_rows(j)], out.at[0, u], out_recv.at[u])

    def own_piece(slot, j):
        return (slot == c) & (4 * c + j == t)

    own = pl.ds(pl.multiple_of(c * ROWS, ROWS), ROWS)

    def kv_copy(slot, i):
        return pltpu.make_async_remote_copy(
            kv.at[slot, i, own],
            kv.at[slot, i, own],
            kv_send.at[slot, i],
            kv_recv.at[slot, i],
            device_id=partner,
            device_id_type=MESH,
        )

    def kv_arrival(slot, i):
        other = pl.ds(pl.multiple_of((1 - c) * ROWS, ROWS), ROWS)
        return pltpu.make_async_remote_copy(
            kv.at[slot, i, other],
            kv.at[slot, i, other],
            kv_send.at[slot, i],
            kv_recv.at[slot, i],
            device_id=partner,
            device_id_type=MESH,
        )

    def rim_copy(slot):
        return pltpu.make_async_remote_copy(
            rim_out.at[slot],
            rim_in.at[slot],
            rim_send.at[slot],
            rim_recv.at[slot],
            device_id=partner,
            device_id_type=MESH,
        )

    def run_slot(slot, carry):
        mine = slot == c

        def ready(*ids):
            for i in ids:

                @pl.when(mine)
                def _(i=i):
                    local(i).wait()

                @pl.when(jnp.logical_not(mine))
                def _(i=i):
                    pull(i, slot).wait_recv()

        length = lengths[u]

        @pl.when(slot == 0)
        def _():
            for j in range(PIECES):
                itself = (k == 0) & (4 * c + j == t)

                @pl.when(itself)
                def _():
                    for v in range(UTTS):

                        @pl.when(t == 2 * v + 1)
                        def _(v=v):
                            frame_local(v).wait()

                @pl.when(jnp.logical_not(itself))
                def _(j=j):
                    forward(j).wait_recv()

        ready(0, 7)
        act[...] = normed(xs[slot].astype(F32), vec[slot, 0]).astype(BF16)

        def up_tile(n, carry):
            cols = pl.ds(pl.multiple_of(n * 512, 512), 512)
            v = dot(act[...], w_up[slot, :, cols])
            wide[:, cols] = (v * sigmoid(v)).astype(BF16)
            return carry

        lax.fori_loop(0, 4, up_tile, 0)
        ready(8)

        def down_tile(n, carry):
            cols = pl.ds(pl.multiple_of(n * 512, 512), 512)
            v = dot(wide[...], w_down[slot, :, cols])
            res[:, cols] = xs[slot, :, cols].astype(F32) + 0.5 * v
            return carry

        lax.fori_loop(0, 2, down_tile, 0)
        ready(1, 9, 10)
        act[...] = normed(res[...], vec[slot, 1]).astype(BF16)

        def proj_tile(w, store):
            def tile(n, carry):
                cols = pl.ds(pl.multiple_of(n * 512, 512), 512)
                store(cols, dot(act[...], w[slot, :, cols]).astype(BF16))
                return carry

            lax.fori_loop(0, 2, tile, 0)

        def store_key(cols, v):
            kv[slot, 0, own, cols] = v

        def store_value(cols, v):
            kv[slot, 1, own, cols] = v

        def store_query(cols, v):
            wide[:, cols] = v * jnp.asarray(0.125, BF16)

        proj_tile(w_key, store_key)
        kv_copy(slot, 0).start()
        proj_tile(w_value, store_value)
        kv_copy(slot, 1).start()
        ready(11)
        proj_tile(w_query, store_query)
        kv_arrival(slot, 0).wait_recv()
        kv_arrival(slot, 1).wait_recv()

        seen = lax.broadcasted_iota(jnp.int32, (1, LEN), 1) < length
        bias = jnp.where(seen, 0.0, -1e30).astype(F32)
        low = lax.broadcasted_iota(jnp.int32, (ROWS, 128), 1) < 64

        def head_pair(g, carry):
            cols = pl.ds(pl.multiple_of(g * 128, 128), 128)
            q = wide[:, cols]
            keys = kv[slot, 0, :, cols]
            values = kv[slot, 1, :, cols]
            mixed = []
            for part in (low, jnp.logical_not(low)):
                q_head = jnp.where(part, q, jnp.zeros_like(q))
                scores = lax.dot_general(
                    q_head, keys, (((1,), (1,)), ((), ())), preferred_element_type=F32
                )
                scores = scores + bias
                peak = jnp.max(scores, axis=-1, keepdims=True)
                weights = jnp.exp(scores - peak)
                total = jnp.sum(weights, axis=-1, keepdims=True)
                mixed.append(dot(weights.astype(BF16), values) * (1.0 / total))
            act[:, cols] = jnp.where(low, mixed[0], mixed[1]).astype(BF16)
            return carry

        lax.fori_loop(0, HEADS // 2, head_pair, 0)
        ready(12)

        def out_tile(n, carry):
            cols = pl.ds(pl.multiple_of(n * 512, 512), 512)
            res[:, cols] = res[:, cols] + dot(act[...], w_out[slot, :, cols])
            return carry

        lax.fori_loop(0, 2, out_tile, 0)
        ready(2, 13)
        wide[:, :D] = normed(res[...], vec[slot, 2]).astype(BF16)
        row = c * ROWS + lax.broadcasted_iota(jnp.int32, (ROWS, 256), 0)
        keep = (row < length).astype(F32)

        def glu_tile(n, carry):
            base = pl.multiple_of(n * 256, 256)
            value = dot(wide[:, :D], w_expand[slot, :, pl.ds(base, 256)])
            gate = dot(wide[:, :D], w_expand[slot, :, pl.ds(base + D, 256)])
            glu = (value * sigmoid(gate) * keep).astype(BF16)
            edge = jnp.where(c == 0, glu[ROWS - 16 :], glu[:16])
            rim_out[slot, :, pl.ds(base, 256)] = edge
            glu = glu.astype(F32)
            padded[2 * n, pl.ds(16, ROWS), :] = glu[:, :128]
            padded[2 * n + 1, pl.ds(16, ROWS), :] = glu[:, 128:]
            return carry

        lax.fori_loop(0, 4, glu_tile, 0)
        rim_copy(slot).start()
        ready(3, 4, 6)
        rim_copy(slot).wait_recv()
        for n in range(8):
            got = rim_in[slot, :, n * 128 : (n + 1) * 128].astype(F32)
            zero = jnp.zeros_like(got)
            padded[n, pl.ds(0, 16), :] = jnp.where(c == 0, zero, got)
            padded[n, pl.ds(16 + ROWS, 16), :] = jnp.where(c == 0, got, zero)

        def conv_tile(i, carry):
            n = i // 2
            half = lax.rem(i, 2) * 128
            cols = pl.ds(pl.multiple_of(n * 128, 128), 128)
            weights = [taps[slot, pl.ds(j, 1), cols] for j in range(TAPS)]
            sums = [None] * 16
            for o in range(1, 8 * 15 + TAPS + 1):
                v = padded[n, pl.ds(half + o, 8), :]
                for b in range(16):
                    j = o - 1 - 8 * b
                    if 0 <= j < TAPS:
                        term = v * weights[j]
                        sums[b] = term if sums[b] is None else sums[b] + term
            for b in range(16):
                depth[pl.ds(pl.multiple_of(half + 8 * b, 8), 8), cols] = sums[b]
            return carry

        lax.fori_loop(0, 16, conv_tile, 0)
        shifted = normed(depth[...], vec[slot, 3]) + vec[slot, 4]
        act[...] = (shifted * sigmoid(shifted)).astype(BF16)
        ready(14, 5)
        for h in range(2):
            rows = pl.ds(h * 128, 128)
            closing = res[rows, :] + dot(act[rows, :], w_shrink[slot])
            xs[slot + 1, rows, :] = normed(closing, vec[slot, 5]).astype(BF16)
            for j in (2 * h, 2 * h + 1):

                @pl.when((slot == 1) & (k < STAGES - 1))
                def _(j=j):
                    forward(j).start()

                @pl.when(own_piece(slot, j))
                def _(j=j):
                    scatter_local(slot, j).start()

                @pl.when(jnp.logical_not(own_piece(slot, j)))
                def _(j=j):
                    scatter(slot, j).start()

        return carry

    @pl.when(active)
    def _():
        lax.fori_loop(0, 2, run_slot, 0)
        for i in ORDER:
            push(i).wait_send()
        for slot in range(2):
            for i in range(2):
                kv_copy(slot, i).wait_send()
            rim_copy(slot).wait_send()
            for j in range(PIECES):

                @pl.when(jnp.logical_not(own_piece(slot, j)))
                def _(slot=slot, j=j):
                    scatter(slot, j).wait_send()

        @pl.when(k < STAGES - 1)
        def _():
            for j in range(PIECES):
                forward(j).wait_send()

    for v in range(UTTS):

        @pl.when(sends_frames & (t != 2 * v + 1))
        def _(v=v):
            frame_copy(v).wait_send()

    for v in range(UTTS):
        itself = (t == 2 * v + side) & (c == t // 4)
        landed = out.at[0, v]

        @pl.when(itself)
        def _(v=v, landed=landed):
            pltpu.make_async_copy(xs.at[0, piece_rows(0)], landed, out_recv.at[v]).wait()

        @pl.when(jnp.logical_not(itself))
        def _(v=v, landed=landed):
            pltpu.make_async_remote_copy(
                landed, landed, out_send.at[0, 0], out_recv.at[v], device_id=partner, device_id_type=MESH
            ).wait_recv()


def body(
    frames,
    lengths,
    ffn_gain,
    ffn_up,
    ffn_down,
    attn_gain,
    query_weight,
    key_weight,
    value_weight,
    out_weight,
    conv_gain,
    expand_weight,
    depth_weight,
    depth_gain,
    norm_shift,
    shrink_weight,
    final_gain,
):
    anywhere = pl.BlockSpec(memory_space=pl.ANY)
    dma = pltpu.SemaphoreType.DMA
    return pl.pallas_call(
        block_kernel,
        name="conformer",
        out_shape=jax.ShapeDtypeStruct((1, UTTS, PIECE, D), BF16),
        in_specs=[pl.BlockSpec(memory_space=pltpu.SMEM)] + [anywhere] * 16,
        out_specs=anywhere,
        scratch_shapes=[pltpu.VMEM((2,) + shape, BF16) for shape in SHAPES]
        + [
            pltpu.VMEM((2, 6, 1, D), F32),
            pltpu.VMEM((2, TAPS, D), F32),
            pltpu.VMEM((3, ROWS, D), BF16),
            pltpu.VMEM((ROWS, D), BF16),
            pltpu.VMEM((ROWS, FF), BF16),
            pltpu.VMEM((ROWS, D), F32),
            pltpu.VMEM((2, 2, LEN, D), BF16),
            pltpu.VMEM((2, 16, D), BF16),
            pltpu.VMEM((2, 16, D), BF16),
            pltpu.VMEM((8, ROWS + 32, 128), F32),
            pltpu.VMEM((ROWS, D), F32),
            dma((15,)),
            dma((15,)),
            dma((15,)),
            dma((PIECES,)),
            dma((PIECES,)),
            dma((2, PIECES)),
            dma((UTTS,)),
            dma((2, 2)),
            dma((2, 2)),
            dma((2,)),
            dma((2,)),
            dma((UTTS,)),
        ],
        compiler_params=pltpu.CompilerParams(
            has_side_effects=True, vmem_limit_bytes=67043328
        ),
    )(
        lengths,
        frames,
        ffn_gain,
        attn_gain,
        conv_gain,
        depth_gain,
        norm_shift,
        final_gain,
        depth_weight,
        ffn_up,
        ffn_down,
        key_weight,
        value_weight,
        query_weight,
        out_weight,
        expand_weight,
        shrink_weight,
    )


def solution(mesh):
    return jax.shard_map(
        body,
        mesh=mesh,
        in_specs=(
            P(None, "tm", None),
            P(),
            P("section", None),
            P("section", None, None),
            P("section", None, None),
            P("section", None),
            P("section", None, None),
            P("section", None, None),
            P("section", None, None),
            P("section", None, None),
            P("section", None),
            P("section", None, None),
            P("section", None, None),
            P("section", None),
            P("section", None),
            P("section", None, None),
            P("section", None),
        ),
        out_specs=P("section", None, "tm", None),
        check_vma=False,
    )
```

time: 1500 us -> 488 us (0.33)
  waiting for transfers between devices: 732 us -> 0 us
  starting transfers between devices: 543 us -> 0 us
  Pallas kernels: 0 us -> 484 us
  local copies, waits for them, and re-layouts: 89.2 us -> 3.45 us
  matrix products: 70 us -> 0 us
  other arithmetic: 52.2 us -> 0 us
    ppermute x57 -> x0, waiting for transfers between devices: 492 us -> none  [the longest x19 482 us: passed_along(): return lax.ppermute(shard, axis, pairs)]
    pallas_call x0 -> x1, Pallas kernels: none -> 484 us  [body(): pl.pallas_call(block_kernel, name='conformer', out_shape=jax.ShapeDtypeSt...]
    all_to_all x76 -> x0, starting transfers between devices: 399 us -> none  [the longest x19 104 us: tick(): lax.all_to_all(queries, 'tm', split_axis=1, concat_axis=0, tiled=True)]
    all_to_all x76 -> x0, waiting for transfers between devices: 240 us -> none  [the longest x19 69.7 us: tick(): lax.all_to_all(grouped, 'tm', split_axis=0, concat_axis=1, tiled=True)]
    ppermute x57 -> x0, starting transfers between devices: 144 us -> none  [the longest x19 65.3 us: extended(): before = lax.ppermute(last, axis, up)]
    dot_general x36 -> x0, matrix products: 70 us -> none  [the longest x4 21 us: project(): jnp.dot(inner, w_down, preferred_element_type=jnp.float32)]
    all_to_all x57 -> x0, local copies, waits for them, and re-layouts: 38.1 us -> none  [the longest x19 12.7 us: tick(): lax.all_to_all(keys, 'tm', split_axis=1, concat_axis=0, tiled=True)]
    reduce_sum x51 -> x0, other arithmetic: 30.8 us -> none  [the longest x19 13.6 us: tick(): jnp.sum(jnp.where(jnp.arange(micro, dtype=jnp.int32) == slot, lengths, 0))]
  transfers between devices with their start and end apart: 133 -> 0, of which waited for: 114 -> 0; matrix products, arithmetic and copies ran while one was open for 5% -> 0% of each run, Pallas kernels for 0% -> 0%
where the time goes in v1:
time: 488 us
  Pallas kernels  484 us (99%)
    pallas_call x1, Pallas kernels, body(): pl.pallas_call(block_kernel, name='conformer', out_shape=jax.ShapeDtypeSt...  484 us

profile of v1, /device:TPU:111, one launch (start us, length us, event | category | flops | bytes accessed | tf_op | source)
XLA Modules:
  0.0 487.6 jit_solution(11823539363561663376)
XLA Ops:
  0.0 1.6 copy.18.depth_weight
  1.6 484.2 %conformer.1 = bf16[1,4,64,1024]{3,2,1,0:T(8,128)(2,1)} custom-call(s32[4]{0:T(128)} %lengths.1, bf16[4,64,1024]{2,1,0:T(8,128)(2,1)} %frames.1, f32[1,1024]{1,0:T(1,128)} %ffn_gain.1, f32[1,1024]{1,0:T(1,128)} %attn_gain.1, f32[1,1024]{1,0:T(1,128)} %conv_gain.1, f32[1,1024]{1,0:T(1,128)} %depth_gain.1, f32[1,1024]{1,0:T(1,128)} %norm_shift.1, ...), custom_call_target="tpu_custom_call" | custom-call | tf_op jit(solution)/shard_map/conformer/pallas_call | solution.py:476
  485.8 1.9 copy.20

commit v2 on v1

--- a/solution.py
+++ b/solution.py
@@ -21,6 +21,7 @@
 STAGES = 8
 PIECE = 64
 PIECES = ROWS // PIECE
+QUERY_SCALE = 0.125 * 1.4426950408889634
 SHAPES = ((D, FF), (FF, D), (D, D), (D, D), (D, D), (D, D), (D, 2 * D), (D, D))
 
 
@@ -75,6 +76,7 @@
     kv,
     rim_out,
     rim_in,
+    bias,
     padded,
     depth,
     local_sem,
@@ -131,7 +133,7 @@
             ref, ref, push_sem.at[i], pull_sem.at[i], device_id=partner, device_id_type=MESH
         )
 
-    ORDER = (0, 7, 8, 1, 9, 10, 11, 12, 2, 13, 3, 4, 6, 14, 5)
+    ORDER = (0, 7, 8, 1, 9, 10, 11, 12, 2, 6, 13, 3, 4, 14, 5)
 
     @pl.when(active)
     def _():
@@ -266,41 +268,41 @@
         ready(0, 7)
         act[...] = normed(xs[slot].astype(F32), vec[slot, 0]).astype(BF16)
 
-        def up_tile(n, carry):
-            cols = pl.ds(pl.multiple_of(n * 512, 512), 512)
+        def up_tile(n):
+            cols = pl.ds(n * 512, 512)
             v = dot(act[...], w_up[slot, :, cols])
             wide[:, cols] = (v * sigmoid(v)).astype(BF16)
-            return carry
-
-        lax.fori_loop(0, 4, up_tile, 0)
+
+        for n in range(4):
+            up_tile(n)
         ready(8)
 
-        def down_tile(n, carry):
-            cols = pl.ds(pl.multiple_of(n * 512, 512), 512)
+        def down_tile(n):
+            cols = pl.ds(n * 512, 512)
             v = dot(wide[...], w_down[slot, :, cols])
             res[:, cols] = xs[slot, :, cols].astype(F32) + 0.5 * v
-            return carry
-
-        lax.fori_loop(0, 2, down_tile, 0)
+
+        for n in range(2):
+            down_tile(n)
         ready(1, 9, 10)
         act[...] = normed(res[...], vec[slot, 1]).astype(BF16)
 
         def proj_tile(w, store):
-            def tile(n, carry):
-                cols = pl.ds(pl.multiple_of(n * 512, 512), 512)
-                store(cols, dot(act[...], w[slot, :, cols]).astype(BF16))
-                return carry
-
-            lax.fori_loop(0, 2, tile, 0)
+            def tile(n):
+                cols = pl.ds(n * 512, 512)
+                store(cols, dot(act[...], w[slot, :, cols]))
+
+            for n in range(2):
+                tile(n)
 
         def store_key(cols, v):
-            kv[slot, 0, own, cols] = v
+            kv[slot, 0, own, cols] = v.astype(BF16)
 
         def store_value(cols, v):
-            kv[slot, 1, own, cols] = v
+            kv[slot, 1, own, cols] = v.astype(BF16)
 
         def store_query(cols, v):
-            wide[:, cols] = v * jnp.asarray(0.125, BF16)
+            wide[:, cols] = (v * QUERY_SCALE).astype(BF16)
 
         proj_tile(w_key, store_key)
         kv_copy(slot, 0).start()
@@ -311,83 +313,92 @@
         kv_arrival(slot, 0).wait_recv()
         kv_arrival(slot, 1).wait_recv()
 
-        seen = lax.broadcasted_iota(jnp.int32, (1, LEN), 1) < length
-        bias = jnp.where(seen, 0.0, -1e30).astype(F32)
         low = lax.broadcasted_iota(jnp.int32, (ROWS, 128), 1) < 64
-
-        def head_pair(g, carry):
-            cols = pl.ds(pl.multiple_of(g * 128, 128), 128)
+        one = jnp.where(lax.broadcasted_iota(jnp.int32, (ROWS, 128), 1) == 0, 1.0, 0.0).astype(BF16)
+        ones = jnp.ones((LEN, 128), BF16)
+
+        def pair_scores(g):
+            cols = pl.ds(g * 128, 128)
             q = wide[:, cols]
-            keys = kv[slot, 0, :, cols]
-            values = kv[slot, 1, :, cols]
-            mixed = []
-            for part in (low, jnp.logical_not(low)):
-                q_head = jnp.where(part, q, jnp.zeros_like(q))
-                scores = lax.dot_general(
-                    q_head, keys, (((1,), (1,)), ((), ())), preferred_element_type=F32
-                )
-                scores = scores + bias
-                peak = jnp.max(scores, axis=-1, keepdims=True)
-                weights = jnp.exp(scores - peak)
-                total = jnp.sum(weights, axis=-1, keepdims=True)
-                mixed.append(dot(weights.astype(BF16), values) * (1.0 / total))
-            act[:, cols] = jnp.where(low, mixed[0], mixed[1]).astype(BF16)
-            return carry
-
-        lax.fori_loop(0, HEADS // 2, head_pair, 0)
+            none = jnp.zeros_like(q)
+            stacked = jnp.concatenate(
+                [
+                    jnp.concatenate([jnp.where(low, q, none), one], axis=1),
+                    jnp.concatenate([jnp.where(low, none, q), one], axis=1),
+                ],
+                axis=0,
+            )
+            keys = jnp.concatenate([kv[slot, 0, :, cols], bias[...]], axis=1)
+            return lax.dot_general(
+                stacked, keys, (((1,), (1,)), ((), ())), preferred_element_type=F32
+            )
+
+        def pair_context(g, scores):
+            cols = pl.ds(g * 128, 128)
+            peak = jnp.max(scores, axis=-1, keepdims=True)
+            weights = jnp.exp2(scores - peak).astype(BF16)
+            values = jnp.concatenate([kv[slot, 1, :, cols], ones], axis=1)
+            mixed = dot(weights, values)
+            total = jnp.where(low, mixed[:ROWS, 128:], mixed[ROWS:, 128:])
+            mixed = jnp.where(low, mixed[:ROWS, :128], mixed[ROWS:, :128])
+            act[:, cols] = (mixed / total).astype(BF16)
+
+        scores = pair_scores(0)
+        for g in range(HEADS // 2):
+            later = pair_scores(g + 1) if g + 1 < HEADS // 2 else None
+            pair_context(g, scores)
+            scores = later
         ready(12)
 
-        def out_tile(n, carry):
-            cols = pl.ds(pl.multiple_of(n * 512, 512), 512)
+        def out_tile(n):
+            cols = pl.ds(n * 512, 512)
             res[:, cols] = res[:, cols] + dot(act[...], w_out[slot, :, cols])
-            return carry
-
-        lax.fori_loop(0, 2, out_tile, 0)
-        ready(2, 13)
+
+        for n in range(2):
+            out_tile(n)
+        ready(2, 13, 6)
         wide[:, :D] = normed(res[...], vec[slot, 2]).astype(BF16)
         row = c * ROWS + lax.broadcasted_iota(jnp.int32, (ROWS, 256), 0)
         keep = (row < length).astype(F32)
 
-        def glu_tile(n, carry):
-            base = pl.multiple_of(n * 256, 256)
-            value = dot(wide[:, :D], w_expand[slot, :, pl.ds(base, 256)])
-            gate = dot(wide[:, :D], w_expand[slot, :, pl.ds(base + D, 256)])
+        def glu_tile(n):
+            value = dot(wide[:, :D], w_expand[slot, :, pl.ds(n * 256, 256)])
+            gate = dot(wide[:, :D], w_expand[slot, :, pl.ds(n * 256 + D, 256)])
             glu = (value * sigmoid(gate) * keep).astype(BF16)
-            edge = jnp.where(c == 0, glu[ROWS - 16 :], glu[:16])
-            rim_out[slot, :, pl.ds(base, 256)] = edge
+            rim_out[slot, :, pl.ds(n * 256, 256)] = jnp.where(c == 0, glu[ROWS - 16 :], glu[:16])
             glu = glu.astype(F32)
             padded[2 * n, pl.ds(16, ROWS), :] = glu[:, :128]
             padded[2 * n + 1, pl.ds(16, ROWS), :] = glu[:, 128:]
-            return carry
-
-        lax.fori_loop(0, 4, glu_tile, 0)
-        rim_copy(slot).start()
-        ready(3, 4, 6)
-        rim_copy(slot).wait_recv()
-        for n in range(8):
-            got = rim_in[slot, :, n * 128 : (n + 1) * 128].astype(F32)
-            zero = jnp.zeros_like(got)
-            padded[n, pl.ds(0, 16), :] = jnp.where(c == 0, zero, got)
-            padded[n, pl.ds(16 + ROWS, 16), :] = jnp.where(c == 0, got, zero)
-
-        def conv_tile(i, carry):
-            n = i // 2
-            half = lax.rem(i, 2) * 128
-            cols = pl.ds(pl.multiple_of(n * 128, 128), 128)
+
+        def conv_rows(n, base, blocks):
+            cols = pl.ds(n * 128, 128)
             weights = [taps[slot, pl.ds(j, 1), cols] for j in range(TAPS)]
-            sums = [None] * 16
-            for o in range(1, 8 * 15 + TAPS + 1):
-                v = padded[n, pl.ds(half + o, 8), :]
-                for b in range(16):
+            sums = [None] * blocks
+            for o in range(1, 8 * (blocks - 1) + TAPS + 1):
+                v = padded[n, pl.ds(base + o, 8), :]
+                for b in range(blocks):
                     j = o - 1 - 8 * b
                     if 0 <= j < TAPS:
                         term = v * weights[j]
                         sums[b] = term if sums[b] is None else sums[b] + term
-            for b in range(16):
-                depth[pl.ds(pl.multiple_of(half + 8 * b, 8), 8), cols] = sums[b]
-            return carry
-
-        lax.fori_loop(0, 16, conv_tile, 0)
+            for b in range(blocks):
+                depth[pl.ds(base + 8 * b, 8), cols] = sums[b]
+
+        for n in range(5):
+            if n < 4:
+                glu_tile(n)
+            if n > 0:
+                for i in (2 * n - 2, 2 * n - 1):
+                    conv_rows(i, 0, 16)
+                    conv_rows(i, 128, 16)
+        rim_copy(slot).start()
+        ready(3, 4)
+        rim_copy(slot).wait_recv()
+        inner_rim = pl.ds(pl.multiple_of((1 - c) * (ROWS + 16), 16), 16)
+        edge = pl.multiple_of((1 - c) * (ROWS - 16), 16)
+        for n in range(8):
+            padded[n, inner_rim, :] = rim_in[slot, :, n * 128 : (n + 1) * 128].astype(F32)
+            conv_rows(n, edge, 2)
         shifted = normed(depth[...], vec[slot, 3]) + vec[slot, 4]
         act[...] = (shifted * sigmoid(shifted)).astype(BF16)
         ready(14, 5)
@@ -413,6 +424,11 @@
 
     @pl.when(active)
     def _():
+        seen = lax.broadcasted_iota(jnp.int32, (LEN, 128), 0) < lengths[u]
+        bias[...] = jnp.where(seen, 0.0, -1e30).astype(BF16)
+        for n in range(8):
+            padded[n, pl.ds(0, 16), :] = jnp.zeros((16, 128), F32)
+            padded[n, pl.ds(16 + ROWS, 16), :] = jnp.zeros((16, 128), F32)
         lax.fori_loop(0, 2, run_slot, 0)
         for i in ORDER:
             push(i).wait_send()
@@ -490,6 +506,7 @@
             pltpu.VMEM((2, 2, LEN, D), BF16),
             pltpu.VMEM((2, 16, D), BF16),
             pltpu.VMEM((2, 16, D), BF16),
+            pltpu.VMEM((LEN, 128), BF16),
             pltpu.VMEM((8, ROWS + 32, 128), F32),
             pltpu.VMEM((ROWS, D), F32),
             dma((15,)),

time: 488 us -> 403 us (0.83)
  Pallas kernels: 484 us -> 399 us
    pallas_call x1, Pallas kernels: 484 us -> 399 us  [body(): pl.pallas_call(block_kernel, name='conformer', out_shape=jax.ShapeDtypeSt...]
where the time goes in v2:
time: 403 us
  Pallas kernels  399 us (99%)
    pallas_call x1, Pallas kernels, body(): pl.pallas_call(block_kernel, name='conformer', out_shape=jax.ShapeDtypeSt...  399 us

profile of v2, /device:TPU:111, one launch (start us, length us, event | category | flops | bytes accessed | tf_op | source)
XLA Modules:
  0.0 402.6 jit_solution(13186843220523604138)
XLA Ops:
  0.0 1.6 copy.18.depth_weight
  1.6 399.1 %conformer.1 = bf16[1,4,64,1024]{3,2,1,0:T(8,128)(2,1)} custom-call(s32[4]{0:T(128)} %lengths.1, bf16[4,64,1024]{2,1,0:T(8,128)(2,1)} %frames.1, f32[1,1024]{1,0:T(1,128)} %ffn_gain.1, f32[1,1024]{1,0:T(1,128)} %attn_gain.1, f32[1,1024]{1,0:T(1,128)} %conv_gain.1, f32[1,1024]{1,0:T(1,128)} %depth_gain.1, f32[1,1024]{1,0:T(1,128)} %norm_shift.1, ...), custom_call_target="tpu_custom_call" | custom-call | tf_op jit(solution)/shard_map/conformer/pallas_call | solution.py:492
  400.7 1.9 copy.20

commit v3 on v2

--- a/solution.py
+++ b/solution.py
@@ -21,6 +21,7 @@
 STAGES = 8
 PIECE = 64
 PIECES = ROWS // PIECE
+HALF = ROWS // 2
 QUERY_SCALE = 0.125 * 1.4426950408889634
 SHAPES = ((D, FF), (FF, D), (D, D), (D, D), (D, D), (D, D), (D, 2 * D), (D, D))
 
@@ -201,26 +202,17 @@
 
     own = pl.ds(pl.multiple_of(c * ROWS, ROWS), ROWS)
 
+    def kv_part(slot, i, rows):
+        ref = kv.at[slot, i // 2, rows, pl.ds((i % 2) * 512, 512)]
+        return pltpu.make_async_remote_copy(
+            ref, ref, kv_send.at[slot, i], kv_recv.at[slot, i], device_id=partner, device_id_type=MESH
+        )
+
     def kv_copy(slot, i):
-        return pltpu.make_async_remote_copy(
-            kv.at[slot, i, own],
-            kv.at[slot, i, own],
-            kv_send.at[slot, i],
-            kv_recv.at[slot, i],
-            device_id=partner,
-            device_id_type=MESH,
-        )
+        return kv_part(slot, i, own)
 
     def kv_arrival(slot, i):
-        other = pl.ds(pl.multiple_of((1 - c) * ROWS, ROWS), ROWS)
-        return pltpu.make_async_remote_copy(
-            kv.at[slot, i, other],
-            kv.at[slot, i, other],
-            kv_send.at[slot, i],
-            kv_recv.at[slot, i],
-            device_id=partner,
-            device_id_type=MESH,
-        )
+        return kv_part(slot, i, pl.ds(pl.multiple_of((1 - c) * ROWS, ROWS), ROWS))
 
     def rim_copy(slot):
         return pltpu.make_async_remote_copy(
@@ -248,70 +240,53 @@
 
         length = lengths[u]
 
-        @pl.when(slot == 0)
-        def _():
-            for j in range(PIECES):
-                itself = (k == 0) & (4 * c + j == t)
-
-                @pl.when(itself)
-                def _():
-                    for v in range(UTTS):
-
-                        @pl.when(t == 2 * v + 1)
-                        def _(v=v):
-                            frame_local(v).wait()
-
-                @pl.when(jnp.logical_not(itself))
-                def _(j=j):
-                    forward(j).wait_recv()
-
-        ready(0, 7)
-        act[...] = normed(xs[slot].astype(F32), vec[slot, 0]).astype(BF16)
-
-        def up_tile(n):
-            cols = pl.ds(n * 512, 512)
-            v = dot(act[...], w_up[slot, :, cols])
-            wide[:, cols] = (v * sigmoid(v)).astype(BF16)
-
-        for n in range(4):
-            up_tile(n)
-        ready(8)
-
-        def down_tile(n):
-            cols = pl.ds(n * 512, 512)
-            v = dot(wide[...], w_down[slot, :, cols])
-            res[:, cols] = xs[slot, :, cols].astype(F32) + 0.5 * v
-
-        for n in range(2):
-            down_tile(n)
+        def input_ready(j):
+            itself = (k == 0) & (4 * c + j == t)
+
+            @pl.when(itself)
+            def _():
+                for v in range(UTTS):
+
+                    @pl.when(t == 2 * v + 1)
+                    def _(v=v):
+                        frame_local(v).wait()
+
+            @pl.when(jnp.logical_not(itself))
+            def _():
+                forward(j).wait_recv()
+
+        ready(0, 7, 8)
+        for h in range(2):
+            rows = pl.ds(h * HALF, HALF)
+
+            @pl.when(slot == 0)
+            def _(h=h):
+                for j in range(h * PIECES // 2, (h + 1) * PIECES // 2):
+                    input_ready(j)
+
+            first = normed(xs[slot, rows].astype(F32), vec[slot, 0]).astype(BF16)
+            act[rows] = first
+            for n in range(4):
+                cols = pl.ds(n * 512, 512)
+                v = dot(act[rows], w_up[slot, :, cols])
+                wide[rows, cols] = (v * sigmoid(v)).astype(BF16)
+            for n in range(2):
+                cols = pl.ds(n * 512, 512)
+                v = dot(wide[rows], w_down[slot, :, cols])
+                res[rows, cols] = xs[slot, rows, cols].astype(F32) + 0.5 * v
         ready(1, 9, 10)
         act[...] = normed(res[...], vec[slot, 1]).astype(BF16)
-
-        def proj_tile(w, store):
-            def tile(n):
-                cols = pl.ds(n * 512, 512)
-                store(cols, dot(act[...], w[slot, :, cols]))
-
-            for n in range(2):
-                tile(n)
-
-        def store_key(cols, v):
-            kv[slot, 0, own, cols] = v.astype(BF16)
-
-        def store_value(cols, v):
-            kv[slot, 1, own, cols] = v.astype(BF16)
-
-        def store_query(cols, v):
-            wide[:, cols] = (v * QUERY_SCALE).astype(BF16)
-
-        proj_tile(w_key, store_key)
-        kv_copy(slot, 0).start()
-        proj_tile(w_value, store_value)
-        kv_copy(slot, 1).start()
+        for i in range(4):
+            cols = pl.ds((i // 2) * 512, 512)
+            w = (w_key, w_value)[i % 2]
+            kv[slot, i % 2, own, cols] = dot(act[...], w[slot, :, cols]).astype(BF16)
+            kv_copy(slot, 2 * (i % 2) + i // 2).start()
         ready(11)
-        proj_tile(w_query, store_query)
+        for n in range(2):
+            cols = pl.ds(n * 512, 512)
+            wide[:, cols] = (dot(act[...], w_query[slot, :, cols]) * QUERY_SCALE).astype(BF16)
         kv_arrival(slot, 0).wait_recv()
-        kv_arrival(slot, 1).wait_recv()
+        kv_arrival(slot, 2).wait_recv()
 
         low = lax.broadcasted_iota(jnp.int32, (ROWS, 128), 1) < 64
         one = jnp.where(lax.broadcasted_iota(jnp.int32, (ROWS, 128), 1) == 0, 1.0, 0.0).astype(BF16)
@@ -345,6 +320,9 @@
 
         scores = pair_scores(0)
         for g in range(HEADS // 2):
+            if g == 3:
+                kv_arrival(slot, 1).wait_recv()
+                kv_arrival(slot, 3).wait_recv()
             later = pair_scores(g + 1) if g + 1 < HEADS // 2 else None
             pair_context(g, scores)
             scores = later
@@ -387,11 +365,12 @@
         for n in range(5):
             if n < 4:
                 glu_tile(n)
+            if n == 3:
+                rim_copy(slot).start()
             if n > 0:
                 for i in (2 * n - 2, 2 * n - 1):
                     conv_rows(i, 0, 16)
                     conv_rows(i, 128, 16)
-        rim_copy(slot).start()
         ready(3, 4)
         rim_copy(slot).wait_recv()
         inner_rim = pl.ds(pl.multiple_of((1 - c) * (ROWS + 16), 16), 16)
@@ -399,13 +378,13 @@
         for n in range(8):
             padded[n, inner_rim, :] = rim_in[slot, :, n * 128 : (n + 1) * 128].astype(F32)
             conv_rows(n, edge, 2)
-        shifted = normed(depth[...], vec[slot, 3]) + vec[slot, 4]
-        act[...] = (shifted * sigmoid(shifted)).astype(BF16)
         ready(14, 5)
         for h in range(2):
-            rows = pl.ds(h * 128, 128)
-            closing = res[rows, :] + dot(act[rows, :], w_shrink[slot])
-            xs[slot + 1, rows, :] = normed(closing, vec[slot, 5]).astype(BF16)
+            rows = pl.ds(h * HALF, HALF)
+            shifted = normed(depth[rows], vec[slot, 3]) + vec[slot, 4]
+            act[rows] = (shifted * sigmoid(shifted)).astype(BF16)
+            closing = res[rows] + dot(act[rows], w_shrink[slot])
+            xs[slot + 1, rows] = normed(closing, vec[slot, 5]).astype(BF16)
             for j in (2 * h, 2 * h + 1):
 
                 @pl.when((slot == 1) & (k < STAGES - 1))
@@ -433,7 +412,7 @@
         for i in ORDER:
             push(i).wait_send()
         for slot in range(2):
-            for i in range(2):
+            for i in range(4):
                 kv_copy(slot, i).wait_send()
             rim_copy(slot).wait_send()
             for j in range(PIECES):
@@ -516,8 +495,8 @@
             dma((PIECES,)),
             dma((2, PIECES)),
             dma((UTTS,)),
-            dma((2, 2)),
-            dma((2, 2)),
+            dma((2, 4)),
+            dma((2, 4)),
             dma((2,)),
             dma((2,)),
             dma((UTTS,)),

time: 403 us -> 374 us (0.928)
  Pallas kernels: 399 us -> 370 us
    pallas_call x1, Pallas kernels: 399 us -> 370 us  [body(): pl.pallas_call(block_kernel, name='conformer', out_shape=jax.ShapeDtypeSt...]
where the time goes in v3:
time: 374 us; the launch traced here: 373 us
  Pallas kernels  370 us (99%)
    pallas_call x1, Pallas kernels, body(): pl.pallas_call(block_kernel, name='conformer', out_shape=jax.ShapeDtypeSt...  370 us

profile of v3, /device:TPU:111, one launch (start us, length us, event | category | flops | bytes accessed | tf_op | source)
XLA Modules:
  0.0 373.3 jit_solution(13002458701116858306)
XLA Ops:
  0.0 1.6 copy.18.depth_weight
  1.6 369.9 %conformer.1 = bf16[1,4,64,1024]{3,2,1,0:T(8,128)(2,1)} custom-call(s32[4]{0:T(128)} %lengths.1, bf16[4,64,1024]{2,1,0:T(8,128)(2,1)} %frames.1, f32[1,1024]{1,0:T(1,128)} %ffn_gain.1, f32[1,1024]{1,0:T(1,128)} %attn_gain.1, f32[1,1024]{1,0:T(1,128)} %conv_gain.1, f32[1,1024]{1,0:T(1,128)} %depth_gain.1, f32[1,1024]{1,0:T(1,128)} %norm_shift.1, ...), custom_call_target="tpu_custom_call" | custom-call | tf_op jit(solution)/shard_map/conformer/pallas_call | solution.py:471
  371.5 1.9 copy.20

commit v4 on v3

--- a/solution.py
+++ b/solution.py
@@ -73,13 +73,14 @@
     xs,
     act,
     wide,
-    res,
+    sums,
     kv,
     rim_out,
     rim_in,
     bias,
     padded,
-    depth,
+    via_x,
+    via_z,
     local_sem,
     push_sem,
     pull_sem,
@@ -92,7 +93,12 @@
     rim_send,
     rim_recv,
     frame_send,
+    via_send,
+    via_recv,
+    hand_send,
+    hand_recv,
 ):
+    res, depth = sums.at[0], sums.at[1]
     s = lax.axis_index("section")
     t = lax.axis_index("tm")
     k = s // 2
@@ -134,6 +140,11 @@
             ref, ref, push_sem.at[i], pull_sem.at[i], device_id=partner, device_id_type=MESH
         )
 
+    lead = (k == 0) & (c == 0)
+
+    def pushed(i):
+        return jnp.logical_not(lead) if i in (0, 7, 8) else k >= 0
+
     ORDER = (0, 7, 8, 1, 9, 10, 11, 12, 2, 6, 13, 3, 4, 14, 5)
 
     @pl.when(active)
@@ -141,33 +152,36 @@
         for i in ORDER:
             local(i).start()
         for i in ORDER:
-            push(i).start()
+
+            @pl.when(pushed(i))
+            def _(i=i):
+                push(i).start()
+
+
+    frame_rows = xs.at[t // 4, pl.ds(pl.multiple_of(lax.rem(t, 4) * PIECE, PIECE), PIECE)]
 
     def frame_copy(v):
         return pltpu.make_async_remote_copy(
             frames.at[v],
-            xs.at[0, pl.ds(pl.multiple_of(lax.rem(t, 4) * PIECE, PIECE), PIECE)],
+            frame_rows,
             frame_send.at[v],
-            x_recv.at[lax.rem(t, 4)],
-            device_id={"section": s, "tm": 2 * v + 1},
+            x_recv.at[t],
+            device_id={"section": 0, "tm": 2 * v + 1},
             device_id_type=MESH,
         )
 
     def frame_local(v):
-        return pltpu.make_async_copy(
-            frames.at[v],
-            xs.at[0, pl.ds(pl.multiple_of(lax.rem(t, 4) * PIECE, PIECE), PIECE)],
-            x_recv.at[lax.rem(t, 4)],
-        )
+        return pltpu.make_async_copy(frames.at[v], frame_rows, x_recv.at[t])
 
     sends_frames = (k == 0) & (t // 4 == c)
     for v in range(UTTS):
-
-        @pl.when(sends_frames & (t != 2 * v + 1))
+        to_itself = (c == 0) & (t == 2 * v + 1)
+
+        @pl.when(sends_frames & jnp.logical_not(to_itself))
         def _(v=v):
             frame_copy(v).start()
 
-        @pl.when(sends_frames & (t == 2 * v + 1))
+        @pl.when(sends_frames & to_itself)
         def _(v=v):
             frame_local(v).start()
 
@@ -184,6 +198,50 @@
             device_id_type=MESH,
         )
 
+    def relayed(src, dst, send, recv, section, tm):
+        return pltpu.make_async_remote_copy(
+            src, dst, send, recv, device_id={"section": lax.rem(section + 16, 16), "tm": tm}, device_id_type=MESH
+        )
+
+    even = lax.rem(k, 2) == 0
+    first_piece = xs.at[0, pl.ds(0, PIECE)]
+    last_first = xs.at[2, pl.ds(0, PIECE)]
+
+    def leave_x():
+        return relayed(last_first, via_x, x_send.at[0], via_recv.at[0], s, 2 * u)
+
+    def leave_z():
+        return relayed(last_first, via_z, x_send.at[0], via_recv.at[1], s + 4, 2 * u + 1)
+
+    def pass_x():
+        return relayed(via_x, via_x, via_send.at[0], via_recv.at[0], s + 2, 2 * u + 1)
+
+    def land_x():
+        return relayed(via_x, first_piece, via_send.at[0], x_recv.at[0], s, 2 * u)
+
+    def land_z():
+        return relayed(via_z, first_piece, via_send.at[1], x_recv.at[0], s - 2, 2 * u + 1)
+
+    idle = jnp.logical_not(active)
+
+    @pl.when(idle & even)
+    def _():
+        pass_x().wait_recv()
+        pass_x().start()
+        pass_x().wait_send()
+
+    @pl.when(idle & jnp.logical_not(even))
+    def _():
+        @pl.when(k >= 3)
+        def _():
+            leave_z().wait_recv()
+            land_z().start()
+            land_z().wait_send()
+
+        pass_x().wait_recv()
+        land_x().start()
+        land_x().wait_send()
+
     def scatter(slot, j):
         return pltpu.make_async_remote_copy(
             xs.at[slot + 1, piece_rows(j)],
@@ -214,6 +272,11 @@
     def kv_arrival(slot, i):
         return kv_part(slot, i, pl.ds(pl.multiple_of((1 - c) * ROWS, ROWS), ROWS))
 
+    def hand_over():
+        return pltpu.make_async_remote_copy(
+            depth, res, hand_send, hand_recv, device_id=partner, device_id_type=MESH
+        )
+
     def rim_copy(slot):
         return pltpu.make_async_remote_copy(
             rim_out.at[slot],
@@ -241,31 +304,36 @@
         length = lengths[u]
 
         def input_ready(j):
-            itself = (k == 0) & (4 * c + j == t)
+            itself = lead & (j == t) & (t < 4)
 
             @pl.when(itself)
             def _():
-                for v in range(UTTS):
-
-                    @pl.when(t == 2 * v + 1)
-                    def _(v=v):
-                        frame_local(v).wait()
+                frame_local(u).wait()
 
             @pl.when(jnp.logical_not(itself))
             def _():
-                forward(j).wait_recv()
-
-        ready(0, 7, 8)
-        for h in range(2):
-            rows = pl.ds(h * HALF, HALF)
+                pltpu.make_async_remote_copy(
+                    first_piece, first_piece, x_send.at[0], x_recv.at[j], device_id=partner, device_id_type=MESH
+                ).wait_recv()
+
+        opening = (k == 0) & (slot == 0)
+        passes = jnp.where(opening, jnp.where(c == 0, 4, 0), 2)
+
+        @pl.when(jnp.logical_not(opening & (c == 1)))
+        def _():
+            ready(0, 7, 8)
+
+        def feed_forward(i, carry):
+            group = i // 2
+            source = xs.at[slot + group]
+            rows = pl.ds(pl.multiple_of(lax.rem(i, 2) * HALF, HALF), HALF)
 
             @pl.when(slot == 0)
-            def _(h=h):
-                for j in range(h * PIECES // 2, (h + 1) * PIECES // 2):
-                    input_ready(j)
-
-            first = normed(xs[slot, rows].astype(F32), vec[slot, 0]).astype(BF16)
-            act[rows] = first
+            def _():
+                input_ready(2 * i)
+                input_ready(2 * i + 1)
+
+            act[rows] = normed(source[rows].astype(F32), vec[slot, 0]).astype(BF16)
             for n in range(4):
                 cols = pl.ds(n * 512, 512)
                 v = dot(act[rows], w_up[slot, :, cols])
@@ -273,7 +341,19 @@
             for n in range(2):
                 cols = pl.ds(n * 512, 512)
                 v = dot(wide[rows], w_down[slot, :, cols])
-                res[rows, cols] = xs[slot, rows, cols].astype(F32) + 0.5 * v
+                sums[group, rows, cols] = source[rows, cols].astype(F32) + 0.5 * v
+            return carry
+
+        lax.fori_loop(0, passes, feed_forward, 0)
+
+        @pl.when(opening & (c == 0))
+        def _():
+            hand_over().start()
+
+        @pl.when(opening & (c == 1))
+        def _():
+            hand_over().wait_recv()
+
         ready(1, 9, 10)
         act[...] = normed(res[...], vec[slot, 1]).astype(BF16)
         for i in range(4):
@@ -335,6 +415,11 @@
         for n in range(2):
             out_tile(n)
         ready(2, 13, 6)
+
+        @pl.when(opening & (c == 0))
+        def _():
+            hand_over().wait_send()
+
         wide[:, :D] = normed(res[...], vec[slot, 2]).astype(BF16)
         row = c * ROWS + lax.broadcasted_iota(jnp.int32, (ROWS, 256), 0)
         keep = (row < length).astype(F32)
@@ -351,16 +436,16 @@
         def conv_rows(n, base, blocks):
             cols = pl.ds(n * 128, 128)
             weights = [taps[slot, pl.ds(j, 1), cols] for j in range(TAPS)]
-            sums = [None] * blocks
+            total = [None] * blocks
             for o in range(1, 8 * (blocks - 1) + TAPS + 1):
                 v = padded[n, pl.ds(base + o, 8), :]
                 for b in range(blocks):
                     j = o - 1 - 8 * b
                     if 0 <= j < TAPS:
                         term = v * weights[j]
-                        sums[b] = term if sums[b] is None else sums[b] + term
+                        total[b] = term if total[b] is None else total[b] + term
             for b in range(blocks):
-                depth[pl.ds(base + 8 * b, 8), cols] = sums[b]
+                depth[pl.ds(base + 8 * b, 8), cols] = total[b]
 
         for n in range(5):
             if n < 4:
@@ -389,7 +474,18 @@
 
                 @pl.when((slot == 1) & (k < STAGES - 1))
                 def _(j=j):
-                    forward(j).start()
+                    if j == 0:
+
+                        @pl.when(even)
+                        def _():
+                            leave_x().start()
+
+                        @pl.when(jnp.logical_not(even))
+                        def _():
+                            leave_z().start()
+
+                    else:
+                        forward(j).start()
 
                 @pl.when(own_piece(slot, j))
                 def _(j=j):
@@ -410,7 +506,11 @@
             padded[n, pl.ds(16 + ROWS, 16), :] = jnp.zeros((16, 128), F32)
         lax.fori_loop(0, 2, run_slot, 0)
         for i in ORDER:
-            push(i).wait_send()
+
+            @pl.when(pushed(i))
+            def _(i=i):
+                push(i).wait_send()
+
         for slot in range(2):
             for i in range(4):
                 kv_copy(slot, i).wait_send()
@@ -428,7 +528,7 @@
 
     for v in range(UTTS):
 
-        @pl.when(sends_frames & (t != 2 * v + 1))
+        @pl.when(sends_frames & jnp.logical_not((c == 0) & (t == 2 * v + 1)))
         def _(v=v):
             frame_copy(v).wait_send()
 
@@ -481,18 +581,19 @@
             pltpu.VMEM((3, ROWS, D), BF16),
             pltpu.VMEM((ROWS, D), BF16),
             pltpu.VMEM((ROWS, FF), BF16),
-            pltpu.VMEM((ROWS, D), F32),
+            pltpu.VMEM((2, ROWS, D), F32),
             pltpu.VMEM((2, 2, LEN, D), BF16),
             pltpu.VMEM((2, 16, D), BF16),
             pltpu.VMEM((2, 16, D), BF16),
             pltpu.VMEM((LEN, 128), BF16),
             pltpu.VMEM((8, ROWS + 32, 128), F32),
-            pltpu.VMEM((ROWS, D), F32),
+            pltpu.VMEM((PIECE, D), BF16),
+            pltpu.VMEM((PIECE, D), BF16),
             dma((15,)),
             dma((15,)),
             dma((15,)),
             dma((PIECES,)),
-            dma((PIECES,)),
+            dma((2 * PIECES,)),
             dma((2, PIECES)),
             dma((UTTS,)),
             dma((2, 4)),
@@ -500,6 +601,10 @@
             dma((2,)),
             dma((2,)),
             dma((UTTS,)),
+            dma((2,)),
+            dma((2,)),
+            dma,
+            dma,
         ],
         compiler_params=pltpu.CompilerParams(
             has_side_effects=True, vmem_limit_bytes=67043328

time: 374 us -> 383 us (1.024)
  Pallas kernels: 370 us -> 379 us
    pallas_call x1, Pallas kernels: 370 us -> 379 us  [body(): pl.pallas_call(block_kernel, name='conformer', out_shape=jax.ShapeDtypeSt...]
where the time goes in v4:
time: 383 us
  Pallas kernels  379 us (99%)
    pallas_call x1, Pallas kernels, body(): pl.pallas_call(block_kernel, name='conformer', out_shape=jax.ShapeDtypeSt...  379 us

profile of v4, /device:TPU:111, one launch (start us, length us, event | category | flops | bytes accessed | tf_op | source)
XLA Modules:
  0.0 382.8 jit_solution(7104295191883715766)
XLA Ops:
  0.0 1.6 copy.18.depth_weight
  1.6 379.4 %conformer.1 = bf16[1,4,64,1024]{3,2,1,0:T(8,128)(2,1)} custom-call(s32[4]{0:T(128)} %lengths.1, bf16[4,64,1024]{2,1,0:T(8,128)(2,1)} %frames.1, f32[1,1024]{1,0:T(1,128)} %ffn_gain.1, f32[1,1024]{1,0:T(1,128)} %attn_gain.1, f32[1,1024]{1,0:T(1,128)} %conv_gain.1, f32[1,1024]{1,0:T(1,128)} %depth_gain.1, f32[1,1024]{1,0:T(1,128)} %norm_shift.1, ...), custom_call_target="tpu_custom_call" | custom-call | tf_op jit(solution)/shard_map/conformer/pallas_call | solution.py:571
  381.0 1.9 copy.20

commit v5 on v4

--- a/solution.py
+++ b/solution.py
@@ -79,7 +79,6 @@
     rim_in,
     bias,
     padded,
-    via_x,
     via_z,
     local_sem,
     push_sem,
@@ -116,7 +115,7 @@
 
     def sources():
         pairs = [(small[i], vec.at[c, i]) for i in range(6)]
-        pairs += [(depth_weight.at[0], taps.at[c])]
+        pairs += [(depth_weight, taps.at[c])]
         pairs += [(hbm[i].at[0], vmem[i].at[c]) for i in range(8)]
         return pairs
 
@@ -146,16 +145,6 @@
         return jnp.logical_not(lead) if i in (0, 7, 8) else k >= 0
 
     ORDER = (0, 7, 8, 1, 9, 10, 11, 12, 2, 6, 13, 3, 4, 14, 5)
-
-    @pl.when(active)
-    def _():
-        for i in ORDER:
-            local(i).start()
-        for i in ORDER:
-
-            @pl.when(pushed(i))
-            def _(i=i):
-                push(i).start()
 
 
     frame_rows = xs.at[t // 4, pl.ds(pl.multiple_of(lax.rem(t, 4) * PIECE, PIECE), PIECE)]
@@ -185,6 +174,31 @@
         def _(v=v):
             frame_local(v).start()
 
+    LEAD = ((1, 9, 10, 11), (12, 2, 6, 13), (3, 4, 14, 5))
+    MATE = ((0, 7, 8), (1, 9, 10), (11, 12, 2, 6, 13, 3, 4, 14, 5))
+
+    def push_part(part, first):
+        @pl.when(first & (c == 0))
+        def _():
+            for i in LEAD[part]:
+                push(i).start()
+
+        @pl.when(first & (c == 1))
+        def _():
+            for i in MATE[part]:
+                push(i).start()
+
+    @pl.when(active)
+    def _():
+        for i in ORDER:
+            local(i).start()
+        push_part(0, k == 0)
+
+        @pl.when(k > 0)
+        def _():
+            for i in ORDER:
+                push(i).start()
+
     def piece_rows(j):
         return pl.ds(j * PIECE, PIECE)
 
@@ -207,40 +221,19 @@
     first_piece = xs.at[0, pl.ds(0, PIECE)]
     last_first = xs.at[2, pl.ds(0, PIECE)]
 
-    def leave_x():
-        return relayed(last_first, via_x, x_send.at[0], via_recv.at[0], s, 2 * u)
-
     def leave_z():
-        return relayed(last_first, via_z, x_send.at[0], via_recv.at[1], s + 4, 2 * u + 1)
-
-    def pass_x():
-        return relayed(via_x, via_x, via_send.at[0], via_recv.at[0], s + 2, 2 * u + 1)
-
-    def land_x():
-        return relayed(via_x, first_piece, via_send.at[0], x_recv.at[0], s, 2 * u)
+        return relayed(last_first, via_z, x_send.at[0], via_recv, s + 4, 2 * u + 1)
 
     def land_z():
-        return relayed(via_z, first_piece, via_send.at[1], x_recv.at[0], s - 2, 2 * u + 1)
+        return relayed(via_z, first_piece, via_send, x_recv.at[0], s - 2, 2 * u + 1)
 
     idle = jnp.logical_not(active)
 
-    @pl.when(idle & even)
+    @pl.when(idle & jnp.logical_not(even) & (k >= 3))
     def _():
-        pass_x().wait_recv()
-        pass_x().start()
-        pass_x().wait_send()
-
-    @pl.when(idle & jnp.logical_not(even))
-    def _():
-        @pl.when(k >= 3)
-        def _():
-            leave_z().wait_recv()
-            land_z().start()
-            land_z().wait_send()
-
-        pass_x().wait_recv()
-        land_x().start()
-        land_x().wait_send()
+        leave_z().wait_recv()
+        land_z().start()
+        land_z().wait_send()
 
     def scatter(slot, j):
         return pltpu.make_async_remote_copy(
@@ -257,6 +250,15 @@
 
     def own_piece(slot, j):
         return (slot == c) & (4 * c + j == t)
+
+    def emit(slot, j):
+        @pl.when(own_piece(slot, j))
+        def _():
+            scatter_local(slot, j).start()
+
+        @pl.when(jnp.logical_not(own_piece(slot, j)))
+        def _():
+            scatter(slot, j).start()
 
     own = pl.ds(pl.multiple_of(c * ROWS, ROWS), ROWS)
 
@@ -361,6 +363,13 @@
             w = (w_key, w_value)[i % 2]
             kv[slot, i % 2, own, cols] = dot(act[...], w[slot, :, cols]).astype(BF16)
             kv_copy(slot, 2 * (i % 2) + i // 2).start()
+        push_part(1, opening)
+
+        @pl.when(slot == 1)
+        def _():
+            for j in range(PIECES):
+                emit(0, j)
+
         ready(11)
         for n in range(2):
             cols = pl.ds(n * 512, 512)
@@ -435,7 +444,7 @@
 
         def conv_rows(n, base, blocks):
             cols = pl.ds(n * 128, 128)
-            weights = [taps[slot, pl.ds(j, 1), cols] for j in range(TAPS)]
+            weights = [taps[slot, j, :, cols] for j in range(TAPS)]
             total = [None] * blocks
             for o in range(1, 8 * (blocks - 1) + TAPS + 1):
                 v = padded[n, pl.ds(base + o, 8), :]
@@ -452,6 +461,7 @@
                 glu_tile(n)
             if n == 3:
                 rim_copy(slot).start()
+                push_part(2, opening)
             if n > 0:
                 for i in (2 * n - 2, 2 * n - 1):
                     conv_rows(i, 0, 16)
@@ -478,7 +488,7 @@
 
                         @pl.when(even)
                         def _():
-                            leave_x().start()
+                            forward(0).start()
 
                         @pl.when(jnp.logical_not(even))
                         def _():
@@ -487,13 +497,14 @@
                     else:
                         forward(j).start()
 
-                @pl.when(own_piece(slot, j))
+                @pl.when((slot == 1) & (k == STAGES - 1))
                 def _(j=j):
-                    scatter_local(slot, j).start()
-
-                @pl.when(jnp.logical_not(own_piece(slot, j)))
-                def _(j=j):
-                    scatter(slot, j).start()
+                    emit(1, j)
+
+        @pl.when((slot == 1) & (k < STAGES - 1))
+        def _():
+            for j in range(PIECES):
+                emit(1, j)
 
         return carry
 
@@ -577,7 +588,7 @@
         scratch_shapes=[pltpu.VMEM((2,) + shape, BF16) for shape in SHAPES]
         + [
             pltpu.VMEM((2, 6, 1, D), F32),
-            pltpu.VMEM((2, TAPS, D), F32),
+            pltpu.VMEM((2, TAPS, 1, D), F32),
             pltpu.VMEM((3, ROWS, D), BF16),
             pltpu.VMEM((ROWS, D), BF16),
             pltpu.VMEM((ROWS, FF), BF16),
@@ -587,7 +598,6 @@
             pltpu.VMEM((2, 16, D), BF16),
             pltpu.VMEM((LEN, 128), BF16),
             pltpu.VMEM((8, ROWS + 32, 128), F32),
-            pltpu.VMEM((PIECE, D), BF16),
             pltpu.VMEM((PIECE, D), BF16),
             dma((15,)),
             dma((15,)),
@@ -601,8 +611,8 @@
             dma((2,)),
             dma((2,)),
             dma((UTTS,)),
-            dma((2,)),
-            dma((2,)),
+            dma,
+            dma,
             dma,
             dma,
         ],
@@ -618,7 +628,7 @@
         depth_gain,
         norm_shift,
         final_gain,
-        depth_weight,
+        jnp.transpose(depth_weight, (1, 0, 2)),
         ffn_up,
         ffn_down,
         key_weight,

time: 383 us -> 369 us (0.963)
  Pallas kernels: 379 us -> 367 us
    pallas_call x1, Pallas kernels: 379 us -> 367 us  [body(): pl.pallas_call(block_kernel, name='conformer', out_shape=jax.ShapeDtypeSt...]
where the time goes in v5:
time: 369 us
  Pallas kernels  367 us (99%)
    pallas_call x1, Pallas kernels, body(): pl.pallas_call(block_kernel, name='conformer', out_shape=jax.ShapeDtypeSt...  367 us

profile of v5, /device:TPU:111, one launch (start us, length us, event | category | flops | bytes accessed | tf_op | source)
XLA Modules:
  0.0 368.7 jit_solution(4958869371848511757)
XLA Ops:
  0.0 366.8 %conformer.1 = bf16[1,4,64,1024]{3,2,1,0:T(8,128)(2,1)} custom-call(s32[4]{0:T(128)} %lengths.1, bf16[4,64,1024]{2,1,0:T(8,128)(2,1)} %frames.1, f32[1,1024]{1,0:T(1,128)} %ffn_gain.1, f32[1,1024]{1,0:T(1,128)} %attn_gain.1, f32[1,1024]{1,0:T(1,128)} %conv_gain.1, f32[1,1024]{1,0:T(1,128)} %depth_gain.1, f32[1,1024]{1,0:T(1,128)} %norm_shift.1, ...), custom_call_target="tpu_custom_call" | custom-call | tf_op jit(solution)/shard_map/conformer/pallas_call | solution.py:582
  366.8 1.9 copy.19

commit v6 on v5

--- a/solution.py
+++ b/solution.py
@@ -159,20 +159,12 @@
             device_id_type=MESH,
         )
 
-    def frame_local(v):
-        return pltpu.make_async_copy(frames.at[v], frame_rows, x_recv.at[t])
-
-    sends_frames = (k == 0) & (t // 4 == c)
-    for v in range(UTTS):
-        to_itself = (c == 0) & (t == 2 * v + 1)
-
-        @pl.when(sends_frames & jnp.logical_not(to_itself))
-        def _(v=v):
+    sends_frames = (k == 1) & (t // 4 == c)
+
+    @pl.when(sends_frames)
+    def _():
+        for v in range(UTTS):
             frame_copy(v).start()
-
-        @pl.when(sends_frames & to_itself)
-        def _(v=v):
-            frame_local(v).start()
 
     LEAD = ((1, 9, 10, 11), (12, 2, 6, 13), (3, 4, 14, 5))
     MATE = ((0, 7, 8), (1, 9, 10), (11, 12, 2, 6, 13, 3, 4, 14, 5))
@@ -289,10 +281,10 @@
             device_id_type=MESH,
         )
 
-    def run_slot(slot, carry):
+    def run_slot(slot, carry, fast):
         mine = slot == c
 
-        def ready(*ids):
+        def wait_for(*ids):
             for i in ids:
 
                 @pl.when(mine)
@@ -303,32 +295,36 @@
                 def _(i=i):
                     pull(i, slot).wait_recv()
 
+        if fast:
+            wait_for(*range(15))
+
+        def ready(*ids):
+            if not fast:
+                wait_for(*ids)
+
         length = lengths[u]
 
         def input_ready(j):
-            itself = lead & (j == t) & (t < 4)
-
-            @pl.when(itself)
-            def _():
-                frame_local(u).wait()
-
-            @pl.when(jnp.logical_not(itself))
-            def _():
-                pltpu.make_async_remote_copy(
-                    first_piece, first_piece, x_send.at[0], x_recv.at[j], device_id=partner, device_id_type=MESH
-                ).wait_recv()
+            pltpu.make_async_remote_copy(
+                first_piece, first_piece, x_send.at[0], x_recv.at[j], device_id=partner, device_id_type=MESH
+            ).wait_recv()
 
         opening = (k == 0) & (slot == 0)
         passes = jnp.where(opening, jnp.where(c == 0, 4, 0), 2)
 
-        @pl.when(jnp.logical_not(opening & (c == 1)))
-        def _():
-            ready(0, 7, 8)
+        def when_opening(condition):
+            return pl.when(opening & condition) if not fast else (lambda f: None)
+
+        if not fast:
+
+            @pl.when(jnp.logical_not(opening & (c == 1)))
+            def _():
+                ready(0, 7, 8)
 
         def feed_forward(i, carry):
             group = i // 2
             source = xs.at[slot + group]
-            rows = pl.ds(pl.multiple_of(lax.rem(i, 2) * HALF, HALF), HALF)
+            rows = pl.ds(i * HALF, HALF) if fast else pl.ds(pl.multiple_of(lax.rem(i, 2) * HALF, HALF), HALF)
 
             @pl.when(slot == 0)
             def _():
@@ -346,13 +342,17 @@
                 sums[group, rows, cols] = source[rows, cols].astype(F32) + 0.5 * v
             return carry
 
-        lax.fori_loop(0, passes, feed_forward, 0)
-
-        @pl.when(opening & (c == 0))
+        if fast:
+            for i in range(2):
+                feed_forward(i, 0)
+        else:
+            lax.fori_loop(0, passes, feed_forward, 0)
+
+        @when_opening(c == 0)
         def _():
             hand_over().start()
 
-        @pl.when(opening & (c == 1))
+        @when_opening(c == 1)
         def _():
             hand_over().wait_recv()
 
@@ -363,7 +363,8 @@
             w = (w_key, w_value)[i % 2]
             kv[slot, i % 2, own, cols] = dot(act[...], w[slot, :, cols]).astype(BF16)
             kv_copy(slot, 2 * (i % 2) + i // 2).start()
-        push_part(1, opening)
+        if not fast:
+            push_part(1, opening)
 
         @pl.when(slot == 1)
         def _():
@@ -425,7 +426,7 @@
             out_tile(n)
         ready(2, 13, 6)
 
-        @pl.when(opening & (c == 0))
+        @when_opening(c == 0)
         def _():
             hand_over().wait_send()
 
@@ -461,7 +462,8 @@
                 glu_tile(n)
             if n == 3:
                 rim_copy(slot).start()
-                push_part(2, opening)
+                if not fast:
+                    push_part(2, opening)
             if n > 0:
                 for i in (2 * n - 2, 2 * n - 1):
                     conv_rows(i, 0, 16)
@@ -515,7 +517,15 @@
         for n in range(8):
             padded[n, pl.ds(0, 16), :] = jnp.zeros((16, 128), F32)
             padded[n, pl.ds(16 + ROWS, 16), :] = jnp.zeros((16, 128), F32)
-        lax.fori_loop(0, 2, run_slot, 0)
+
+        @pl.when(k == 0)
+        def _():
+            lax.fori_loop(0, 2, functools.partial(run_slot, fast=False), 0)
+
+        @pl.when(k > 0)
+        def _():
+            lax.fori_loop(0, 2, functools.partial(run_slot, fast=True), 0)
+
         for i in ORDER:
 
             @pl.when(pushed(i))
@@ -537,10 +547,9 @@
             for j in range(PIECES):
                 forward(j).wait_send()
 
-    for v in range(UTTS):
-
-        @pl.when(sends_frames & jnp.logical_not((c == 0) & (t == 2 * v + 1)))
-        def _(v=v):
+    @pl.when(sends_frames)
+    def _():
+        for v in range(UTTS):
             frame_copy(v).wait_send()
 
     for v in range(UTTS):

time: 369 us -> 367 us (level)
  no operation moved by 1% of the time
where the time goes in v6:
time: 367 us; the launch traced here: 366 us
  Pallas kernels  365 us (99%)
    pallas_call x1, Pallas kernels, body(): pl.pallas_call(block_kernel, name='conformer', out_shape=jax.ShapeDtypeSt...  365 us

profile of v6, /device:TPU:111, one launch (start us, length us, event | category | flops | bytes accessed | tf_op | source)
XLA Modules:
  0.0 366.4 jit_solution(13435943733243661983)
XLA Ops:
  0.0 364.6 %conformer.1 = bf16[1,4,64,1024]{3,2,1,0:T(8,128)(2,1)} custom-call(s32[4]{0:T(128)} %lengths.1, bf16[4,64,1024]{2,1,0:T(8,128)(2,1)} %frames.1, f32[1,1024]{1,0:T(1,128)} %ffn_gain.1, f32[1,1024]{1,0:T(1,128)} %attn_gain.1, f32[1,1024]{1,0:T(1,128)} %conv_gain.1, f32[1,1024]{1,0:T(1,128)} %depth_gain.1, f32[1,1024]{1,0:T(1,128)} %norm_shift.1, ...), custom_call_target="tpu_custom_call" | custom-call | tf_op jit(solution)/shard_map/conformer/pallas_call | solution.py:591
  364.6 1.9 copy.19

commit v7 on v6

--- a/solution.py
+++ b/solution.py
@@ -22,6 +22,7 @@
 PIECE = 64
 PIECES = ROWS // PIECE
 HALF = ROWS // 2
+CHUNK = 16
 QUERY_SCALE = 0.125 * 1.4426950408889634
 SHAPES = ((D, FF), (FF, D), (D, D), (D, D), (D, D), (D, D), (D, 2 * D), (D, D))
 
@@ -79,6 +80,7 @@
     rim_in,
     bias,
     padded,
+    via_x,
     via_z,
     local_sem,
     push_sem,
@@ -94,6 +96,8 @@
     frame_send,
     via_send,
     via_recv,
+    chunk_send,
+    chunk_recv,
     hand_send,
     hand_recv,
 ):
@@ -159,12 +163,20 @@
             device_id_type=MESH,
         )
 
-    sends_frames = (k == 1) & (t // 4 == c)
-
-    @pl.when(sends_frames)
-    def _():
-        for v in range(UTTS):
+    def frame_local(v):
+        return pltpu.make_async_copy(frames.at[v], frame_rows, x_recv.at[t])
+
+    sends_frames = (k == 0) & (t // 4 == c)
+    for v in range(UTTS):
+        to_itself = (c == 0) & (t == 2 * v + 1)
+
+        @pl.when(sends_frames & jnp.logical_not(to_itself))
+        def _(v=v):
             frame_copy(v).start()
+
+        @pl.when(sends_frames & to_itself)
+        def _(v=v):
+            frame_local(v).start()
 
     LEAD = ((1, 9, 10, 11), (12, 2, 6, 13), (3, 4, 14, 5))
     MATE = ((0, 7, 8), (1, 9, 10), (11, 12, 2, 6, 13, 3, 4, 14, 5))
@@ -213,6 +225,24 @@
     first_piece = xs.at[0, pl.ds(0, PIECE)]
     last_first = xs.at[2, pl.ds(0, PIECE)]
 
+    def chunk(ref, n):
+        return ref.at[pl.ds(n * CHUNK, CHUNK)]
+
+    def leave_x(n):
+        return relayed(
+            chunk(xs.at[2], n), chunk(via_x, n), x_send.at[0], chunk_recv.at[n], s, 2 * u
+        )
+
+    def pass_x(n):
+        return relayed(
+            chunk(via_x, n), chunk(via_x, n), chunk_send.at[n], chunk_recv.at[n], s + 2, 2 * u + 1
+        )
+
+    def land_x(n):
+        return relayed(
+            chunk(via_x, n), chunk(xs.at[0], n), chunk_send.at[n], x_recv.at[0], s, 2 * u
+        )
+
     def leave_z():
         return relayed(last_first, via_z, x_send.at[0], via_recv, s + 4, 2 * u + 1)
 
@@ -221,11 +251,27 @@
 
     idle = jnp.logical_not(active)
 
-    @pl.when(idle & jnp.logical_not(even) & (k >= 3))
+    @pl.when(idle & even)
     def _():
-        leave_z().wait_recv()
-        land_z().start()
-        land_z().wait_send()
+        for n in range(PIECE // CHUNK):
+            pass_x(n).wait_recv()
+            pass_x(n).start()
+        for n in range(PIECE // CHUNK):
+            pass_x(n).wait_send()
+
+    @pl.when(idle & jnp.logical_not(even))
+    def _():
+        @pl.when(k >= 3)
+        def _():
+            leave_z().wait_recv()
+            land_z().start()
+            land_z().wait_send()
+
+        for n in range(PIECE // CHUNK):
+            pass_x(n).wait_recv()
+            land_x(n).start()
+        for n in range(PIECE // CHUNK):
+            land_x(n).wait_send()
 
     def scatter(slot, j):
         return pltpu.make_async_remote_copy(
@@ -305,9 +351,21 @@
         length = lengths[u]
 
         def input_ready(j):
-            pltpu.make_async_remote_copy(
-                first_piece, first_piece, x_send.at[0], x_recv.at[j], device_id=partner, device_id_type=MESH
-            ).wait_recv()
+            def remote():
+                pltpu.make_async_remote_copy(
+                    first_piece, first_piece, x_send.at[0], x_recv.at[j], device_id=partner, device_id_type=MESH
+                ).wait_recv()
+
+            if fast:
+                remote()
+                return
+            itself = lead & (j == t) & (t < 4)
+
+            @pl.when(itself)
+            def _():
+                frame_local(u).wait()
+
+            pl.when(jnp.logical_not(itself))(remote)
 
         opening = (k == 0) & (slot == 0)
         passes = jnp.where(opening, jnp.where(c == 0, 4, 0), 2)
@@ -342,27 +400,35 @@
                 sums[group, rows, cols] = source[rows, cols].astype(F32) + 0.5 * v
             return carry
 
+        if not fast:
+            lax.fori_loop(0, passes, feed_forward, 0)
+
+        @when_opening(c == 0)
+        def _():
+            hand_over().start()
+
+        @when_opening(c == 1)
+        def _():
+            hand_over().wait_recv()
+
+        ready(1, 9, 10)
+
+        def attention_input(rows, offset, length, share):
+            act[rows] = normed(res[rows], vec[slot, 1]).astype(BF16)
+            mine_rows = pl.ds(pl.multiple_of(c * ROWS + offset, HALF), length)
+            for i in range(4):
+                cols = pl.ds((i // 2) * 512, 512)
+                w = (w_key, w_value)[i % 2]
+                kv[slot, i % 2, mine_rows, cols] = dot(act[rows], w[slot, :, cols]).astype(BF16)
+                if share:
+                    kv_copy(slot, 2 * (i % 2) + i // 2).start()
+
         if fast:
             for i in range(2):
                 feed_forward(i, 0)
+                attention_input(pl.ds(i * HALF, HALF), i * HALF, HALF, i == 1)
         else:
-            lax.fori_loop(0, passes, feed_forward, 0)
-
-        @when_opening(c == 0)
-        def _():
-            hand_over().start()
-
-        @when_opening(c == 1)
-        def _():
-            hand_over().wait_recv()
-
-        ready(1, 9, 10)
-        act[...] = normed(res[...], vec[slot, 1]).astype(BF16)
-        for i in range(4):
-            cols = pl.ds((i // 2) * 512, 512)
-            w = (w_key, w_value)[i % 2]
-            kv[slot, i % 2, own, cols] = dot(act[...], w[slot, :, cols]).astype(BF16)
-            kv_copy(slot, 2 * (i % 2) + i // 2).start()
+            attention_input(pl.ds(0, ROWS), 0, ROWS, True)
         if not fast:
             push_part(1, opening)
 
@@ -490,7 +556,8 @@
 
                         @pl.when(even)
                         def _():
-                            forward(0).start()
+                            for n in range(PIECE // CHUNK):
+                                leave_x(n).start()
 
                         @pl.when(jnp.logical_not(even))
                         def _():
@@ -547,9 +614,10 @@
             for j in range(PIECES):
                 forward(j).wait_send()
 
-    @pl.when(sends_frames)
-    def _():
-        for v in range(UTTS):
+    for v in range(UTTS):
+
+        @pl.when(sends_frames & jnp.logical_not((c == 0) & (t == 2 * v + 1)))
+        def _(v=v):
             frame_copy(v).wait_send()
 
     for v in range(UTTS):
@@ -608,6 +676,7 @@
             pltpu.VMEM((LEN, 128), BF16),
             pltpu.VMEM((8, ROWS + 32, 128), F32),
             pltpu.VMEM((PIECE, D), BF16),
+            pltpu.VMEM((PIECE, D), BF16),
             dma((15,)),
             dma((15,)),
             dma((15,)),
@@ -622,6 +691,8 @@
             dma((UTTS,)),
             dma,
             dma,
+            dma((PIECE // CHUNK,)),
+            dma((PIECE // CHUNK,)),
             dma,
             dma,
         ],

time: 367 us -> 367 us (level)
  no operation moved by 1% of the time
where the time goes in v7:
time: 367 us
  Pallas kernels  365 us (99%)
    pallas_call x1, Pallas kernels, body(): pl.pallas_call(block_kernel, name='conformer', out_shape=jax.ShapeDtypeSt...  365 us

profile of v7, /device:TPU:111, one launch (start us, length us, event | category | flops | bytes accessed | tf_op | source)
XLA Modules:
  0.0 367.0 jit_solution(3018683163906088429)
XLA Ops:
  0.0 365.2 %conformer.1 = bf16[1,4,64,1024]{3,2,1,0:T(8,128)(2,1)} custom-call(s32[4]{0:T(128)} %lengths.1, bf16[4,64,1024]{2,1,0:T(8,128)(2,1)} %frames.1, f32[1,1024]{1,0:T(1,128)} %ffn_gain.1, f32[1,1024]{1,0:T(1,128)} %attn_gain.1, f32[1,1024]{1,0:T(1,128)} %conv_gain.1, f32[1,1024]{1,0:T(1,128)} %depth_gain.1, f32[1,1024]{1,0:T(1,128)} %norm_shift.1, ...), custom_call_target="tpu_custom_call" | custom-call | tf_op jit(solution)/shard_map/conformer/pallas_call | solution.py:659
  365.2 1.9 copy.19

commit v8 on v7

--- a/solution.py
+++ b/solution.py
@@ -426,9 +426,7 @@
         if fast:
             for i in range(2):
                 feed_forward(i, 0)
-                attention_input(pl.ds(i * HALF, HALF), i * HALF, HALF, i == 1)
-        else:
-            attention_input(pl.ds(0, ROWS), 0, ROWS, True)
+        attention_input(pl.ds(0, ROWS), 0, ROWS, True)
         if not fast:
             push_part(1, opening)
 

time: 367 us -> 362 us (0.986)
  Pallas kernels: 365 us -> 360 us
    pallas_call x1, Pallas kernels: 365 us -> 360 us  [body(): pl.pallas_call(block_kernel, name='conformer', out_shape=jax.ShapeDtypeSt...]
where the time goes in v8:
time: 362 us
  Pallas kernels  360 us (99%)
    pallas_call x1, Pallas kernels, body(): pl.pallas_call(block_kernel, name='conformer', out_shape=jax.ShapeDtypeSt...  360 us

profile of v8, /device:TPU:111, one launch (start us, length us, event | category | flops | bytes accessed | tf_op | source)
XLA Modules:
  0.0 361.7 jit_solution(15532066351938995123)
XLA Ops:
  0.0 359.8 %conformer.1 = bf16[1,4,64,1024]{3,2,1,0:T(8,128)(2,1)} custom-call(s32[4]{0:T(128)} %lengths.1, bf16[4,64,1024]{2,1,0:T(8,128)(2,1)} %frames.1, f32[1,1024]{1,0:T(1,128)} %ffn_gain.1, f32[1,1024]{1,0:T(1,128)} %attn_gain.1, f32[1,1024]{1,0:T(1,128)} %conv_gain.1, f32[1,1024]{1,0:T(1,128)} %depth_gain.1, f32[1,1024]{1,0:T(1,128)} %norm_shift.1, ...), custom_call_target="tpu_custom_call" | custom-call | tf_op jit(solution)/shard_map/conformer/pallas_call | solution.py:657
  359.8 1.9 copy.19
